TPU v7x, 768 devices: a whole 4x8x12 slice. The times are simulated.
768 devices in a mesh: corpus: 192 (over x_hi, y, z), tensor: 4 (over x_lo, core).
Axes of the slice: x: 4 (x_hi: 2, x_lo: 2; x = x_hi * 2 + x_lo), y: 8, z: 12, core: 2. Of those that a mesh axis runs over, the one named last changes fastest.
Arguments:
- q_states: bfloat16 [12288, 4096], P('corpus', 'tensor'), may hold values from -90 to 90
- k_states: bfloat16 [12288, 1024], P('corpus', 'tensor'), may hold values from -9 to 9
- v_states: bfloat16 [12288, 1024], P('corpus', 'tensor'), may hold values from -6 to 6
- residual: bfloat16 [12288, 4096], P('corpus'), may hold values from -170 to 170
- out_weight: bfloat16 [4096, 4096], P('tensor'), may hold values from -0.09375 to 0.09375
- final_gain: float32 [4096], replicated, may hold values from 0.25 to 1.75
- passages: bfloat16 [196608, 4096], P(('corpus', 'tensor')), may hold values from -5 to 5
- lengths: int32 [768], P('corpus'), may hold values from 1 to 16
Outputs:
- scores: float32 [768, 196608], P(None, ('corpus', 'tensor'))
- log_norm: float32 [768], replicated
All inputs are finite; a program needn't handle non-finite values.
Results may differ from a plain program's by a relative error of at most 0.0003.
The roundings to bfloat16 on the way count: a program that leaves them out, or rounds other values in their place, can miss the bound.
Values may be sent and summed in bfloat16 or wider, within the bound.
No kernel may reach another device: no remote copies, remote signals or barrier semaphores. Data moves between devices by JAX's collectives and lax.ppermute only.
A program may use at most 64 MiB of HBM per device.

v0:
```python
import functools
import math

import jax
import jax.numpy as jnp
from jax import lax
from jax.sharding import Mesh
from jax.sharding import PartitionSpec as P

HEAD_DIM = 128
SEQ = 16
TENSOR = ("tensor_0", "tensor_1")
CORPUS = ("corpus_0", "corpus_1", "corpus_2")
CORPUS_TENSOR = ("corpus_0", "corpus_1", "corpus_2", "tensor_0", "tensor_1")


score_scale = 50.0


def copy_for_each(shard, axis):
    length = lax.axis_size(axis)
    return lax.all_to_all(
        jnp.broadcast_to(shard[None], (length, *shard.shape)), axis, 0, 0, tiled=True
    )


def taken_together(shard, axis):
    everything = copy_for_each(shard, axis)
    return jnp.sum(everything, axis=0)


def by_axis(shard, axes):
    return functools.reduce(lax.pmax, axes, shard)


def one_axis_at_a_time(shard, axes):
    for axis in axes:
        shard = lax.psum(shard, axis)
    return shard


def attend_rows(queries, key_rows, value_rows, query_place, lengths):
    query_count = queries.shape[0]
    query_span = queries.shape[1]
    pair_heads = key_rows.shape[2] // HEAD_DIM
    grouped = queries.reshape(query_count, query_span, pair_heads, -1, HEAD_DIM)
    keyed = key_rows.reshape(query_count, SEQ, pair_heads, HEAD_DIM)
    valued = value_rows.reshape(query_count, SEQ, pair_heads, HEAD_DIM)
    logits = jnp.einsum(
        "brkgd,bskd->bkgrs", grouped, keyed, preferred_element_type=jnp.float32
    ) / math.sqrt(HEAD_DIM)
    key_place = lax.broadcasted_iota(jnp.int32, (1, 1, SEQ), 2)
    allowed = (key_place <= query_place[:, :, None]) & (key_place < lengths[:, None, None])
    allowed = allowed[:, None, None, :, :]
    logits = jnp.where(allowed, logits, -1e30)
    highest = jnp.max(logits, axis=-1, keepdims=True)
    weights = jnp.where(allowed, jnp.exp(logits - highest), 0.0)
    attention = (weights / jnp.sum(weights, axis=-1, keepdims=True)).astype(jnp.bfloat16)
    context = jnp.einsum("bkgrs,bskd->brkgd", attention, valued, preferred_element_type=jnp.float32)
    return context.reshape(query_count * query_span, -1).astype(jnp.bfloat16)


def normalize_rows(pooled, final_gain):
    scaled = pooled * final_gain[None, :]
    magnitude = jnp.maximum(jnp.sqrt(jnp.sum(scaled * scaled, axis=1, keepdims=True)), 1.0)
    return (scaled / magnitude).astype(jnp.bfloat16)


def on_device(q_states, k_states, v_states, residual, out_weight, final_gain, passages, lengths):
    query_count = lengths.shape[0]
    places = lax.broadcasted_iota(jnp.int32, (query_count, SEQ), 1)
    picker = (places == (lengths - 1)[:, None]).astype(jnp.float32)
    key_rows = k_states.reshape(query_count, SEQ, -1)
    value_rows = v_states.reshape(query_count, SEQ, -1)
    chosen_query = jnp.sum(
        picker[:, :, None] * q_states.reshape(query_count, SEQ, -1).astype(jnp.float32), axis=1
    )
    chosen_query = chosen_query.astype(jnp.bfloat16)
    context = attend_rows(
        chosen_query[:, None, :], key_rows, value_rows, (lengths - 1)[:, None], lengths
    )
    partial_value = jnp.dot(context, out_weight, preferred_element_type=jnp.float32)
    summed = taken_together(partial_value, TENSOR)
    residual_last = jnp.sum(
        picker[:, :, None] * residual.reshape(query_count, SEQ, -1).astype(jnp.float32), axis=1
    )
    pooled = residual_last + summed
    embed = normalize_rows(pooled, final_gain)
    scores = (
        lax.dot_general(
            lax.all_gather(embed, CORPUS, axis=0, tiled=True),
            passages,
            (((1,), (1,)), ((), ())),
            preferred_element_type=jnp.float32,
        )
        * score_scale
    )
    local_peak = jnp.max(scores, axis=1)
    global_peak = by_axis(local_peak, CORPUS_TENSOR)
    global_total = one_axis_at_a_time(
        jnp.sum(jnp.exp(scores - global_peak[:, None]), axis=1), CORPUS_TENSOR
    )
    return (scores, global_peak + jnp.log(global_total))


def solution(mesh):
    split = Mesh(
        mesh.devices.reshape(2, 8, 12, 2, 2),
        ("corpus_0", "corpus_1", "corpus_2", "tensor_0", "tensor_1"),
    )
    in_specs = (
        P(CORPUS, TENSOR),
        P(CORPUS, TENSOR),
        P(CORPUS, TENSOR),
        P(CORPUS, None),
        P(TENSOR, None),
        P(),
        P(CORPUS_TENSOR, None),
        P(CORPUS),
    )
    out_specs = (P(None, CORPUS_TENSOR), P())
    return jax.shard_map(
        on_device, mesh=split, in_specs=in_specs, out_specs=out_specs, check_vma=False
    )
```

profile of v0, /device:TPU:1, one launch (start us, length us, event | category | flops | bytes accessed | tf_op | source)
XLA Modules:
  0.0 369.1 jit_solution(3079300007970503042)
XLA Ops:
  7.2 0.0 copy-start
  7.2 0.8 broadcast_add_fusion
  8.0 0.7 fusion.15
  8.7 1.0 fusion.5
  9.8 0.8 reshape_reshape.6
  10.5 0.8 reshape_reshape.7
  11.3 0.2 fusion.17
  11.5 0.2 fusion.9
  11.7 0.2 fusion.1
  11.9 0.0 copy-start.1
  11.9 0.0 copy-start.2
  12.0 4.6 %fusion.19 = f32[4,4096]{1,0:T(4,128)S(1)} fusion(bf16[4,1024]{1,0:T(4,128)(2,1)S(1)} %convert_element_type.60, bf16[1024,4096]{1,0:T(8,128)(2,1)} %param.12), kind=kOutput, calls=%fused_computation.36 | convolution fusion | flops 33554432 | bytes 8462336 | tf_op jit(solution)/shard_map/dot_general | solution.py:82
  16.6 0.7 broadcast_in_dim.40
  17.3 13.8 %all-to-all-start = ((f32[4,4,4096]{2,1,0:T(4,128)}), f32[4,4,4096]{2,1,0:T(4,128)S(1)}, u32[]{:S(2)}, u32[]{:S(2)}) async-start(f32[4,4,4096]{2,1,0:T(4,128)} %broadcast_in_dim.40), calls=%async_computation | async-start | bytes 524288 | tf_op jit(solution)/shard_map/all_to_all | solution.py:22
  31.2 0.0 all-gather.3.cloned.1.call-start
  31.2 0.0 copy-done.1
  31.2 0.3 fusion.4
  31.5 4.7 %all-to-all-done = f32[4,4,4096]{2,1,0:T(4,128)S(1)} async-done(((f32[4,4,4096]{2,1,0:T(4,128)}), f32[4,4,4096]{2,1,0:T(4,128)S(1)}, u32[]{:S(2)}, u32[]{:S(2)}) %all-to-all-start) | async-done | bytes 262176 | tf_op jit(solution)/shard_map/all_to_all | solution.py:22
  36.2 0.1 reduce_sum.57
  36.3 0.0 copy-done.2
  36.3 0.1 multiply_reduce_fusion
  36.5 0.7 fusion.8
  37.2 0.0 all-gather.3.cloned.1.call-update
  37.2 199.3 %all-gather.3.cloned.1.call-done = bf16[192,4,4096]{2,1,0:T(4,128)(2,1)} async-done(((bf16[1,4,4096]{2,1,0:T(4,128)(2,1)}), bf16[192,4,4096]{2,1,0:T(4,128)(2,1)}) %all-gather.3.cloned.1.call-update) | async-done | bytes 6291472 | tf_op jit(solution)/shard_map/all_gather | solution.py:91
  236.5 9.7 %reshape.111 = bf16[768,4096]{1,0:T(8,128)(2,1)} reshape(bf16[192,4,4096]{2,1,0:T(4,128)(2,1)} %all-gather.3.cloned.1.call-done) | data formatting | bytes 12582912
  246.2 0.0 copy-done
  246.2 4.6 %fusion.18 = (f32[768]{0:T(1024)S(1)}, f32[768,256]{0,1:T(8,128)S(1)}) fusion(bf16[768,4096]{1,0:T(8,128)(2,1)} %reshape.111, bf16[256,4096]{1,0:T(8,128)(2,1)S(1)} %copy-done), kind=kOutput, calls=%fused_computation.35 | convolution fusion | flops 1611005184 | bytes 9178112 | tf_op jit(solution)/shard_map/dot_general | solution.py:90
  250.8 5.3 %pmax.35 = f32[768]{0:T(1024)S(1)} all-reduce(f32[768]{0:T(1024)S(1)} %get-tuple-element.12), channel_id=1, replica_groups=mesh['corpus_0'=2,'corpus_1'=8,'corpus_2'=12,'tensor_0'=2,'tensor_1'=2] ..., use_global_device_ids=true, to_apply=%region_7.8 | all-reduce | flops 768 | bytes 6144 | tf_op jit(solution)/shard_map/pmax | solution.py:33
  256.1 13.6 %pmax.36 = f32[768]{0:T(1024)S(1)} all-reduce(f32[768]{0:T(1024)S(1)} %pmax.35), channel_id=1, replica_groups=mesh['corpus_0'=2,'corpus_1'=8,'corpus_2'=12,'tensor_0'=2,'tensor_1'=2] ..., use_global_device_ids=true, to_apply=%region_8.9 | all-reduce | flops 768 | bytes 6144 | tf_op jit(solution)/shard_map/pmax | solution.py:33
  269.7 16.0 %pmax.37 = f32[768]{0:T(1024)S(1)} all-reduce(f32[768]{0:T(1024)S(1)} %pmax.36), channel_id=1, replica_groups=mesh['corpus_0'=2,'corpus_1'=8,'corpus_2'=12,'tensor_0'=2,'tensor_1'=2] ..., use_global_device_ids=true, to_apply=%region_9.10 | all-reduce | flops 768 | bytes 6144 | tf_op jit(solution)/shard_map/pmax | solution.py:33
  285.7 3.8 %pmax.38 = f32[768]{0:T(1024)S(1)} all-reduce(f32[768]{0:T(1024)S(1)} %pmax.37), channel_id=1, replica_groups=mesh['corpus_0'=2,'corpus_1'=8,'corpus_2'=12,'tensor_0'=2,'tensor_1'=2] ..., use_global_device_ids=true, to_apply=%region_10.11 | all-reduce | flops 768 | bytes 6144 | tf_op jit(solution)/shard_map/pmax | solution.py:33
  289.5 20.0 %pmax.39 = f32[768]{0:T(1024)S(1)} all-reduce(f32[768]{0:T(1024)S(1)} %pmax.38), channel_id=1, replica_groups=mesh['corpus_0'=2,'corpus_1'=8,'corpus_2'=12,'tensor_0'=2,'tensor_1'=2] ..., use_global_device_ids=true, to_apply=%region_11.12 | all-reduce | flops 768 | bytes 6144 | tf_op jit(solution)/shard_map/pmax | solution.py:33
  309.5 1.1 copy.18
  310.7 0.1 exponential_reduce_fusion
  310.8 5.3 %psum.35 = f32[768]{0:T(1024)S(1)} all-reduce(f32[768]{0:T(1024)S(1)} %exponential_reduce_fusion), channel_id=1, replica_groups=mesh['corpus_0'=2,'corpus_1'=8,'corpus_2'=12,'tensor_0'=2,'tensor_1'=2] ..., use_global_device_ids=true, to_apply=%region_13.14 | all-reduce | flops 768 | bytes 6144 | tf_op jit(solution)/shard_map/psum | solution.py:38
  316.1 11.5 %psum.36 = f32[768]{0:T(1024)S(1)} all-reduce(f32[768]{0:T(1024)S(1)} %psum.35), channel_id=1, replica_groups=mesh['corpus_0'=2,'corpus_1'=8,'corpus_2'=12,'tensor_0'=2,'tensor_1'=2] ..., use_global_device_ids=true, to_apply=%region_14.15 | all-reduce | flops 768 | bytes 6144 | tf_op jit(solution)/shard_map/psum | solution.py:38
  327.6 16.3 %psum.37 = f32[768]{0:T(1024)S(1)} all-reduce(f32[768]{0:T(1024)S(1)} %psum.36), channel_id=1, replica_groups=mesh['corpus_0'=2,'corpus_1'=8,'corpus_2'=12,'tensor_0'=2,'tensor_1'=2] ..., use_global_device_ids=true, to_apply=%region_15.16 | all-reduce | flops 768 | bytes 6144 | tf_op jit(solution)/shard_map/psum | solution.py:38
  343.8 3.9 %psum.38 = f32[768]{0:T(1024)S(1)} all-reduce(f32[768]{0:T(1024)S(1)} %psum.37), channel_id=1, replica_groups=mesh['corpus_0'=2,'corpus_1'=8,'corpus_2'=12,'tensor_0'=2,'tensor_1'=2] ..., use_global_device_ids=true, to_apply=%region_16.17 | all-reduce | flops 768 | bytes 6144 | tf_op jit(solution)/shard_map/psum | solution.py:38
  347.7 13.9 %psum.39 = f32[768]{0:T(1024)S(1)} all-reduce(f32[768]{0:T(1024)S(1)} %psum.38), channel_id=1, replica_groups=mesh['corpus_0'=2,'corpus_1'=8,'corpus_2'=12,'tensor_0'=2,'tensor_1'=2] ..., use_global_device_ids=true, to_apply=%region_17.18 | all-reduce | flops 768 | bytes 6144 | tf_op jit(solution)/shard_map/psum | solution.py:38
  361.6 0.6 log_add_fusion
  (3 shorter events, 0.0 us)
Async XLA Ops:
  7.2 239.0 %copy-start = (bf16[256,4096]{1,0:T(8,128)(2,1)S(1)}, bf16[256,4096]{1,0:T(8,128)(2,1)}, u32[]{:S(2)}) copy-start(bf16[256,4096]{1,0:T(8,128)(2,1)} %param.14) | copy-start | bytes 6291460
  11.9 19.3 %copy-start.1 = (bf16[64,4096]{1,0:T(8,128)(2,1)S(1)}, bf16[64,4096]{1,0:T(8,128)(2,1)}, u32[]{:S(2)}) copy-start(bf16[64,4096]{1,0:T(8,128)(2,1)} %param.11) | copy-start | bytes 1572868
  11.9 24.3 %copy-start.2 = (f32[4096]{0:T(1024)S(1)}, f32[4096]{0:T(1024)}, u32[]{:S(2)}) copy-start(f32[4096]{0:T(1024)} %param.13) | copy-start | bytes 49156
  17.3 18.9 %all-to-all-start = ((f32[4,4,4096]{2,1,0:T(4,128)}), f32[4,4,4096]{2,1,0:T(4,128)S(1)}, u32[]{:S(2)}, u32[]{:S(2)}) async-start(f32[4,4,4096]{2,1,0:T(4,128)} %broadcast_in_dim.40), calls=%async_computation | async-start | bytes 524288 | tf_op jit(solution)/shard_map/all_to_all | solution.py:22
  31.2 205.3 %all-gather.3.cloned.1.call-start = ((), (), s32[]{:S(2)}) async-start(), calls=%async_computation.1 | async-start | bytes 6324224 | tf_op jit(solution)/shard_map/all_gather | solution.py:91
Sparse Core Ops, SparseCore 0:
  38.1 198.3 all-gather.2
where the time goes:
time: 370 us; the launch traced here: 369 us
  waiting for transfers between devices  204 us (55%)
  blocking collectives  110 us (30%)
  between operations  14.1 us (4%)
  starting transfers between devices  13.9 us (4%)
  local copies, waits for them, and re-layouts  13.2 us (4%)
  matrix products  9.67 us (3%)
  other arithmetic  4.69 us (1%)
    all_gather x1, waiting for transfers between devices, on_device(): lax.all_gather(embed, CORPUS, axis=0, tiled=True)  199 us
    pmax x5, blocking collectives, by_axis(): return functools.reduce(lax.pmax, axes, shard)  58.7 us
    psum x5, blocking collectives, one_axis_at_a_time(): shard = lax.psum(shard, axis)  50.8 us
    all_to_all x1, starting transfers between devices, copy_for_each(): lax.all_to_all(jnp.broadcast_to(shard[None], (length, *shard.shape)), axi...  13.8 us
    unnamed x8, local copies, waits for them, and re-layouts  10.9 us
  transfers between devices with their start and end apart: 2, of which 2 were waited for; matrix products, arithmetic and copies ran while one was open for 0% of the time, Pallas kernels for 0%

commit v1 on v0

--- a/solution.py
+++ b/solution.py
@@ -9,34 +9,27 @@
 
 HEAD_DIM = 128
 SEQ = 16
-TENSOR = ("tensor_0", "tensor_1")
-CORPUS = ("corpus_0", "corpus_1", "corpus_2")
-CORPUS_TENSOR = ("corpus_0", "corpus_1", "corpus_2", "tensor_0", "tensor_1")
-
+XH, Y, Z, XL, C = "corpus_0", "corpus_1", "corpus_2", "tensor_0", "tensor_1"
+TENSOR = (XL, C)
+CORPUS = (XH, Y, Z)
+CORPUS_TENSOR = (XH, Y, Z, XL, C)
 
 score_scale = 50.0
 
 
-def copy_for_each(shard, axis):
-    length = lax.axis_size(axis)
+def size_of(axes):
+    return math.prod(lax.axis_size(axis) for axis in axes)
+
+
+def to_all(shard, axes):
+    length = size_of(axes)
     return lax.all_to_all(
-        jnp.broadcast_to(shard[None], (length, *shard.shape)), axis, 0, 0, tiled=True
+        jnp.broadcast_to(shard[None], (length, *shard.shape)), axes, 0, 0, tiled=True
     )
 
 
-def taken_together(shard, axis):
-    everything = copy_for_each(shard, axis)
-    return jnp.sum(everything, axis=0)
-
-
-def by_axis(shard, axes):
-    return functools.reduce(lax.pmax, axes, shard)
-
-
-def one_axis_at_a_time(shard, axes):
-    for axis in axes:
-        shard = lax.psum(shard, axis)
-    return shard
+def swap(array, axis):
+    return lax.ppermute(array, axis, [(0, 1), (1, 0)])
 
 
 def attend_rows(queries, key_rows, value_rows, query_place, lengths):
@@ -66,8 +59,18 @@
     return (scaled / magnitude).astype(jnp.bfloat16)
 
 
+def merge(peaks, totals, axes):
+    peak = jnp.max(peaks, axis=axes, keepdims=True)
+    total = jnp.sum(totals * jnp.exp(peaks - peak), axis=axes)
+    return jnp.squeeze(peak, axes), total
+
+
 def on_device(q_states, k_states, v_states, residual, out_weight, final_gain, passages, lengths):
+    xh, y, z, xl, c = (lax.axis_size(axis) for axis in CORPUS_TENSOR)
+    tensor = xl * c
     query_count = lengths.shape[0]
+    width = out_weight.shape[1]
+    rows = y * z
     places = lax.broadcasted_iota(jnp.int32, (query_count, SEQ), 1)
     picker = (places == (lengths - 1)[:, None]).astype(jnp.float32)
     key_rows = k_states.reshape(query_count, SEQ, -1)
@@ -80,34 +83,69 @@
         chosen_query[:, None, :], key_rows, value_rows, (lengths - 1)[:, None], lengths
     )
     partial_value = jnp.dot(context, out_weight, preferred_element_type=jnp.float32)
-    summed = taken_together(partial_value, TENSOR)
     residual_last = jnp.sum(
         picker[:, :, None] * residual.reshape(query_count, SEQ, -1).astype(jnp.float32), axis=1
     )
-    pooled = residual_last + summed
+    first = lax.axis_index(TENSOR) == 0
+    partial_value = partial_value + jnp.where(first, residual_last, 0.0)
+
+    terms = jnp.broadcast_to(partial_value[None], (xh, tensor, width)).reshape(xh * tensor, width)
+    terms = lax.all_to_all(terms, (XH, XL, C), 0, 0, tiled=True)
+    pooled = jnp.sum(terms.reshape(xh, tensor, width), axis=1)
     embed = normalize_rows(pooled, final_gain)
-    scores = (
-        lax.dot_general(
-            lax.all_gather(embed, CORPUS, axis=0, tiled=True),
-            passages,
-            (((1,), (1,)), ((), ())),
-            preferred_element_type=jnp.float32,
+
+    held, embed = lax.optimization_barrier((passages, embed))
+    across = swap(held, XL)
+    partner = swap(held, C)
+    across_partner = swap(across, C)
+
+    one_z = to_all(embed[0:1], (Z,))
+    two_y = to_all(embed[1:2], (Y,))
+    one = to_all(one_z.reshape(z, width), (Y,)).reshape(rows, width)
+    two = to_all(two_y.reshape(y, width), (Z,)).reshape(rows, width)
+    gathered = jnp.concatenate([one, two], axis=0)
+
+    def score(block):
+        return (
+            lax.dot_general(
+                gathered, block, (((1,), (1,)), ((), ())), preferred_element_type=jnp.float32
+            )
+            * score_scale
         )
-        * score_scale
+
+    blocks = [[score(held), score(partner)], [score(across), score(across_partner)]]
+    local_peak = functools.reduce(
+        jnp.maximum, [jnp.max(s, axis=1) for pair in blocks for s in pair]
     )
-    local_peak = jnp.max(scores, axis=1)
-    global_peak = by_axis(local_peak, CORPUS_TENSOR)
-    global_total = one_axis_at_a_time(
-        jnp.sum(jnp.exp(scores - global_peak[:, None]), axis=1), CORPUS_TENSOR
+    local_total = sum(
+        jnp.sum(jnp.exp(s - local_peak[:, None]), axis=1) for pair in blocks for s in pair
     )
-    return (scores, global_peak + jnp.log(global_total))
+
+    me_xl, me_c = lax.axis_index(XL), lax.axis_index(C)
+    outgoing = []
+    for a in range(2):
+        for b in range(2):
+            pair = [jnp.where(me_c == b, p[0], p[1]) for p in blocks]
+            outgoing.append(jnp.where(me_xl == a, pair[0], pair[1]))
+    returned = lax.all_to_all(jnp.stack(outgoing), TENSOR, 0, 0, tiled=True)
+
+    pairs = to_all(jnp.stack([local_peak, local_total]), (Z, C)).reshape(z, c, 2, xh * rows)
+    peak, total = merge(pairs[:, :, 0], pairs[:, :, 1], 0)
+    pairs = to_all(jnp.stack([peak, total]), (XH, Y, XL)).reshape(xh * y, xl, 2, c, xh * rows)
+    peak, total = merge(pairs[:, :, 0], pairs[:, :, 1], 0)
+    log_norm = (peak + jnp.log(total)).reshape(tensor, xh * rows)
+
+    def ordered(values):
+        tail = values.shape[2:]
+        one = values[:, :rows].reshape(tensor, y, z, *tail)
+        two = values[:, rows:].reshape(tensor, z, y, *tail).swapaxes(1, 2)
+        return jnp.moveaxis(jnp.stack([one, two]), 1, 3).reshape(xh * rows * tensor, *tail)
+
+    return ordered(returned), ordered(log_norm)
 
 
 def solution(mesh):
-    split = Mesh(
-        mesh.devices.reshape(2, 8, 12, 2, 2),
-        ("corpus_0", "corpus_1", "corpus_2", "tensor_0", "tensor_1"),
-    )
+    split = Mesh(mesh.devices.reshape(2, 8, 12, 2, 2), CORPUS_TENSOR)
     in_specs = (
         P(CORPUS, TENSOR),
         P(CORPUS, TENSOR),

time: 370 us -> 190 us (0.51)
  waiting for transfers between devices: 204 us -> 70.9 us
  blocking collectives: 110 us -> 37.5 us
  starting transfers between devices: 13.9 us -> 46.1 us
  between operations: 14.1 us -> 0.94 us
  matrix products: 9.67 us -> 15.1 us
  other arithmetic: 4.69 us -> 8.53 us
    all_gather x1 -> x0, waiting for transfers between devices: 199 us -> none  [on_device(): lax.all_gather(embed, CORPUS, axis=0, tiled=True)]
    pmax x5 -> x0, blocking collectives: 58.7 us -> none  [by_axis(): return functools.reduce(lax.pmax, axes, shard)]
    all_to_all x1 -> x6, waiting for transfers between devices: 4.75 us -> 61.9 us  [the longest x5 52.6 us: to_all(): lax.all_to_all(jnp.broadcast_to(shard[None], (length, *shard.shape)), axe...]
    psum x5 -> x0, blocking collectives: 50.8 us -> none  [one_axis_at_a_time(): shard = lax.psum(shard, axis)]
    all_to_all x0 -> x2, blocking collectives: none -> 37.5 us  [the longest x1 19.4 us: to_all(): lax.all_to_all(jnp.broadcast_to(shard[None], (length, *shard.shape)), axe...]
    all_to_all x1 -> x6, starting transfers between devices: 13.8 us -> 31.1 us  [the longest x5 25.5 us: to_all(): lax.all_to_all(jnp.broadcast_to(shard[None], (length, *shard.shape)), axe...]
    ppermute x0 -> x3, starting transfers between devices: none -> 15.1 us  [swap(): return lax.ppermute(array, axis, [(0, 1), (1, 0)])]
    unnamed x8, local copies, waits for them, and re-layouts: 10.9 us -> 1.72 us
  transfers between devices with their start and end apart: 2 -> 9, of which waited for: 2 -> 7; matrix products, arithmetic and copies ran while one was open for 0% -> 7% of each run, Pallas kernels for 0% -> 0%
where the time goes in v1:
time: 190 us; the launch traced here: 189 us
  waiting for transfers between devices  70.9 us (37%)
  starting transfers between devices  46.1 us (24%)
  blocking collectives  37.5 us (20%)
  matrix products  15.1 us (8%)
  local copies, waits for them, and re-layouts  10.2 us (5%)
  other arithmetic  8.53 us (4%)
    all_to_all x5, waiting for transfers between devices, to_all(): lax.all_to_all(jnp.broadcast_to(shard[None], (length, *shard.shape)), axe...  52.6 us
    all_to_all x5, starting transfers between devices, to_all(): lax.all_to_all(jnp.broadcast_to(shard[None], (length, *shard.shape)), axe...  25.5 us
    all_to_all x1, blocking collectives, to_all(): lax.all_to_all(jnp.broadcast_to(shard[None], (length, *shard.shape)), axe...  19.4 us
    all_to_all x1, blocking collectives, on_device(): terms = lax.all_to_all(terms, (XH, XL, C), 0, 0, tiled=True)  18.1 us
    ppermute x3, starting transfers between devices, swap(): return lax.ppermute(array, axis, [(0, 1), (1, 0)])  15.1 us
    dot_general x4, matrix products, score(): lax.dot_general(gathered, block, (((1,), (1,)), ((), ())), preferred_elem...  10.1 us
    all_to_all x1, waiting for transfers between devices, on_device(): returned = lax.all_to_all(jnp.stack(outgoing), TENSOR, 0, 0, tiled=True)  9.25 us
    ppermute x3, waiting for transfers between devices, swap(): return lax.ppermute(array, axis, [(0, 1), (1, 0)])  9 us
  transfers between devices with their start and end apart: 9, of which 7 were waited for; matrix products, arithmetic and copies ran while one was open for 7% of the time, Pallas kernels for 0%

profile of v1, /device:TPU:1, one launch (start us, length us, event | category | flops | bytes accessed | tf_op | source)
XLA Modules:
  0.0 189.4 jit_solution(3501790130844022391)
XLA Ops:
  0.6 0.7 broadcast_add_fusion
  1.3 0.7 fusion.20
  2.0 1.0 fusion.5
  3.1 0.8 reshape_reshape.6
  3.8 0.8 reshape_reshape.7
  4.6 0.2 fusion.25
  5.0 0.2 fusion.1
  5.2 1.3 fusion.4
  6.6 4.6 %convolution_add_fusion = f32[4,4096]{1,0:T(4,128)S(1)} fusion(bf16[4,1024]{1,0:T(4,128)(2,1)S(1)} %convert_element_type.58, bf16[1024,4096]{1,0:T(8,128)(2,1)} %param.12, f32[4,4096]{1,0:T(4,128)S(1)} %fusion.4, pred[]{:T(512)S(6)} %eq.36), kind=kOutput, calls=%fused_computation | convolution fusion | flops 33587200 | bytes 8527873 | tf_op jit(solution)/shard_map/dot_general | solution.py:85
  11.4 18.1 %all_to_all.44 = f32[8,1,4096]{2,1,0:T(1,128)S(1)} all-to-all(f32[8,1,4096]{2,1,0:T(1,128)S(1)} %all_to_all.27), channel_id=1, replica_groups=mesh['corpus_0'=2,'corpus_1'=8,'corpus_2'=12,'tensor_0'=2,'tensor_1'=2] ..., dimensions={0} | all-to-all | bytes 262144 | tf_op jit(solution)/shard_map/all_to_all | solution.py:93
  29.5 0.3 reduce.4
  30.5 0.5 broadcast.87
  31.0 1.2 reduce.10
  32.2 0.7 reshape.239
  32.9 7.6 %all-to-all-start.1 = ((bf16[12,2,2048]{2,1,0:T(2,128)(2,1)}), bf16[12,2,2048]{2,1,0:T(2,128)(2,1)S(1)}, u32[]{:S(2)}, u32[]{:S(2)}) async-start(bf16[12,2,2048]{2,1,0:T(2,128)(2,1)} %reshape.239), calls=%async_computation.1 | async-start | bytes 196608 | tf_op jit(solution)/shard_map/all_to_all | solution.py:26
  40.6 1.0 reduce.9
  41.6 0.7 reshape.237
  42.2 8.4 %all-to-all-done.1 = bf16[12,2,2048]{2,1,0:T(2,128)(2,1)S(1)} async-done(((bf16[12,2,2048]{2,1,0:T(2,128)(2,1)}), bf16[12,2,2048]{2,1,0:T(2,128)(2,1)S(1)}, u32[]{:S(2)}, u32[]{:S(2)}) %all-to-all-start.1) | async-done | bytes 98336 | tf_op jit(solution)/shard_map/all_to_all | solution.py:26
  50.6 6.8 %all-to-all-start.3 = ((bf16[8,2,2048]{2,1,0:T(2,128)(2,1)}), bf16[8,2,2048]{2,1,0:T(2,128)(2,1)S(1)}, u32[]{:S(2)}, u32[]{:S(2)}) async-start(bf16[8,2,2048]{2,1,0:T(2,128)(2,1)} %reshape.237), calls=%async_computation.3 | async-start | bytes 131072 | tf_op jit(solution)/shard_map/all_to_all | solution.py:26
  57.6 7.0 %all-to-all-done.3 = bf16[8,2,2048]{2,1,0:T(2,128)(2,1)S(1)} async-done(((bf16[8,2,2048]{2,1,0:T(2,128)(2,1)}), bf16[8,2,2048]{2,1,0:T(2,128)(2,1)S(1)}, u32[]{:S(2)}, u32[]{:S(2)}) %all-to-all-start.3) | async-done | bytes 65568 | tf_op jit(solution)/shard_map/all_to_all | solution.py:26
  64.7 1.1 broadcast_in_dim.98
  65.7 3.6 %all-to-all-start.2 = ((bf16[8,12,4096]{2,1,0:T(8,128)(2,1)}), bf16[8,12,4096]{2,1,0:T(8,128)(2,1)S(1)}, u32[]{:S(2)}, u32[]{:S(2)}) async-start(bf16[8,12,4096]{2,1,0:T(8,128)(2,1)} %broadcast_in_dim.98), calls=%async_computation.2 | async-start | bytes 2097152 | tf_op jit(solution)/shard_map/all_to_all | solution.py:26
  69.3 2.2 %collective-permute-start.1 = (bf16[256,4096]{1,0:T(8,128)(2,1)}, bf16[256,4096]{1,0:T(8,128)(2,1)}, u32[]{:S(2)}, u32[]{:S(2)}) collective-permute-start(bf16[256,4096]{1,0:T(8,128)(2,1)} %param.14), channel_id=1, source_target_pairs={{0,2},{2,0},{1,3},{3,1},{4,6},{6,4},{5,7},{7,5},{8,10},{10,8},{9,1... | collective-permute-start | bytes 6291464 | tf_op jit(solution)/shard_map/ppermute | solution.py:32
  71.7 23.3 %all-to-all-done.2 = bf16[8,12,4096]{2,1,0:T(8,128)(2,1)S(1)} async-done(((bf16[8,12,4096]{2,1,0:T(8,128)(2,1)}), bf16[8,12,4096]{2,1,0:T(8,128)(2,1)S(1)}, u32[]{:S(2)}, u32[]{:S(2)}) %all-to-all-start.2) | async-done | bytes 786464 | tf_op jit(solution)/shard_map/all_to_all | solution.py:26
  95.0 0.9 broadcast_in_dim.102
  95.9 3.7 %all-to-all-start.4 = ((bf16[12,8,4096]{2,1,0:T(8,128)(2,1)}), bf16[12,8,4096]{2,1,0:T(8,128)(2,1)S(1)}, u32[]{:S(2)}, u32[]{:S(2)}) async-start(bf16[12,8,4096]{2,1,0:T(8,128)(2,1)} %broadcast_in_dim.102), calls=%async_computation.4 | async-start | bytes 1572864 | tf_op jit(solution)/shard_map/all_to_all | solution.py:26
  99.6 5.9 %collective-permute-start = (bf16[256,4096]{1,0:T(8,128)(2,1)}, bf16[256,4096]{1,0:T(8,128)(2,1)}, u32[]{:S(2)}, u32[]{:S(2)}) collective-permute-start(bf16[256,4096]{1,0:T(8,128)(2,1)} %param.14), channel_id=1, source_target_pairs={{0,1},{1,0},{2,3},{3,2},{4,5},{5,4},{6,7},{7,6},{8,9},{9,8},{10,11... | collective-permute-start | bytes 6291464 | tf_op jit(solution)/shard_map/ppermute | solution.py:32
  105.5 9.0 %collective-permute-done.1 = bf16[256,4096]{1,0:T(8,128)(2,1)} collective-permute-done((bf16[256,4096]{1,0:T(8,128)(2,1)}, bf16[256,4096]{1,0:T(8,128)(2,1)}, u32[]{:S(2)}, u32[]{:S(2)}) %collective-permute-start.1) | collective-permute-done | bytes 2097184 | tf_op jit(solution)/shard_map/ppermute | solution.py:32
  114.5 7.0 %collective-permute-start.2 = (bf16[256,4096]{1,0:T(8,128)(2,1)}, bf16[256,4096]{1,0:T(8,128)(2,1)}, u32[]{:S(2)}, u32[]{:S(2)}) collective-permute-start(bf16[256,4096]{1,0:T(8,128)(2,1)} %collective-permute-done.1), channel_id=1, source_target_pairs={{0,1},{1,0},{2,3},{3,2},{4,5},{5,4},{6,7},{7,6},{8,9},{9,8},{10,11... | collective-permute-start | bytes 6291464 | tf_op jit(solution)/shard_map/ppermute | solution.py:32
  121.7 5.0 %all-to-all-done.4 = bf16[12,8,4096]{2,1,0:T(8,128)(2,1)S(1)} async-done(((bf16[12,8,4096]{2,1,0:T(8,128)(2,1)}), bf16[12,8,4096]{2,1,0:T(8,128)(2,1)S(1)}, u32[]{:S(2)}, u32[]{:S(2)}) %all-to-all-start.4) | async-done | bytes 786464 | tf_op jit(solution)/shard_map/all_to_all | solution.py:26
  126.7 2.5 %fusion.28 = (f32[192]{0:T(256)S(1)}, f32[192,256]{1,0:T(8,128)S(1)}) fusion(bf16[256,4096]{1,0:T(8,128)(2,1)} %param.14, bf16[96,4096]{1,0:T(8,128)(2,1)S(1)} %bitcast.103, bf16[96,4096]{1,0:T(8,128)(2,1)S(1)} %reshape.224), kind=kOutput, calls=%fused_computation.79 | convolution fusion | flops 405897024 | bytes 3867392 | tf_op jit(solution)/shard_map/dot_general | solution.py:110
  129.2 2.5 %fusion.27 = (f32[192]{0:T(256)S(1)}, f32[192,256]{1,0:T(8,128)S(1)}) fusion(bf16[256,4096]{1,0:T(8,128)(2,1)} %collective-permute-done.1, bf16[96,4096]{1,0:T(8,128)(2,1)S(1)} %bitcast.104, bf16[96,4096]{1,0:T(8,128)(2,1)S(1)} %reshape.224), kind=kOutput, calls=%fused_computation.78 | convolution fusion | flops 405897024 | bytes 3867392 | tf_op jit(solution)/shard_map/dot_general | solution.py:110
  131.7 2.5 %fusion.29 = (f32[192]{0:T(256)S(1)}, f32[192,256]{1,0:T(8,128)S(1)}) fusion(bf16[256,4096]{1,0:T(8,128)(2,1)} %collective-permute-done, bf16[96,4096]{1,0:T(8,128)(2,1)S(1)} %bitcast.105, bf16[96,4096]{1,0:T(8,128)(2,1)S(1)} %reshape.224), kind=kOutput, calls=%fused_computation.80 | convolution fusion | flops 405897024 | bytes 3867392 | tf_op jit(solution)/shard_map/dot_general | solution.py:110
  134.3 2.5 %fusion.26 = (f32[192]{0:T(256)S(1)}, f32[192,256]{1,0:T(8,128)S(1)}) fusion(bf16[256,4096]{1,0:T(8,128)(2,1)} %collective-permute-done.2, bf16[96,4096]{1,0:T(8,128)(2,1)S(1)} %bitcast.106, bf16[96,4096]{1,0:T(8,128)(2,1)S(1)} %reshape.224), kind=kOutput, calls=%fused_computation.77 | convolution fusion | flops 405897024 | bytes 3867392 | tf_op jit(solution)/shard_map/dot_general | solution.py:110
  136.8 0.3 exponential_reduce_fusion.2
  137.2 19.4 %all_to_all.45 = f32[24,2,192]{2,1,0:T(2,128)S(1)} all-to-all(f32[24,2,192]{2,1,0:T(2,128)S(1)} %broadcast_in_dim.103), channel_id=1, replica_groups=mesh['corpus_0'=2,'corpus_1'=8,'corpus_2'=12,'tensor_0'=2,'tensor_1'=2] ..., dimensions={0} | all-to-all | bytes 73728 | tf_op jit(solution)/shard_map/all_to_all | solution.py:26
  156.8 0.7 broadcast_in_dim.105
  157.4 3.9 %all-to-all-start.7 = ((f32[32,2,2,192]{3,2,1,0:T(2,128)}), f32[32,2,2,192]{3,2,1,0:T(2,128)S(1)}, u32[]{:S(2)}, u32[]{:S(2)}) async-start(f32[32,2,2,192]{3,2,1,0:T(2,128)} %broadcast_in_dim.105), calls=%async_computation.7 | async-start | bytes 262144 | tf_op jit(solution)/shard_map/all_to_all | solution.py:26
  161.3 0.9 pad_maximum_fusion.1
  162.2 9.0 %all-to-all-done.7 = f32[32,2,2,192]{3,2,1,0:T(2,128)S(1)} async-done(((f32[32,2,2,192]{3,2,1,0:T(2,128)}), f32[32,2,2,192]{3,2,1,0:T(2,128)S(1)}, u32[]{:S(2)}, u32[]{:S(2)}) %all-to-all-start.7) | async-done | bytes 98336 | tf_op jit(solution)/shard_map/all_to_all | solution.py:26
  171.2 5.6 %all-to-all-start.5 = ((f32[4,192,256]{2,1,0:T(8,128)}), f32[4,192,256]{2,1,0:T(8,128)S(1)}, u32[]{:S(2)}, u32[]{:S(2)}) async-start(f32[4,192,256]{2,1,0:T(8,128)} %pad_maximum_fusion.1), calls=%async_computation.5 | async-start | bytes 1572864 | tf_op jit(solution)/shard_map/all_to_all | solution.py:130
  177.3 0.2 copy.74
  177.5 0.7 reshape.231
  178.2 9.2 %all-to-all-done.5 = f32[4,192,256]{2,1,0:T(8,128)S(1)} async-done(((f32[4,192,256]{2,1,0:T(8,128)}), f32[4,192,256]{2,1,0:T(8,128)S(1)}, u32[]{:S(2)}, u32[]{:S(2)}) %all-to-all-start.5) | async-done | bytes 786464 | tf_op jit(solution)/shard_map/all_to_all | solution.py:130
  187.5 0.3 copy.66
  187.8 0.3 copy.105
  188.0 0.2 maximum_bitcast_fusion
  188.2 1.2 reshape.227
  (39 shorter events, 2.3 us)
Async XLA Ops:
  6.6 23.4 %copy-start = (f32[4096]{0:T(1024)S(1)}, f32[4096]{0:T(1024)}, u32[]{:S(2)}) copy-start(f32[4096]{0:T(1024)} %param.13) | copy-start | bytes 49156
  32.9 17.7 %all-to-all-start.1 = ((bf16[12,2,2048]{2,1,0:T(2,128)(2,1)}), bf16[12,2,2048]{2,1,0:T(2,128)(2,1)S(1)}, u32[]{:S(2)}, u32[]{:S(2)}) async-start(bf16[12,2,2048]{2,1,0:T(2,128)(2,1)} %reshape.239), calls=%async_computation.1 | async-start | bytes 196608 | tf_op jit(solution)/shard_map/all_to_all | solution.py:26
  50.6 14.1 %all-to-all-start.3 = ((bf16[8,2,2048]{2,1,0:T(2,128)(2,1)}), bf16[8,2,2048]{2,1,0:T(2,128)(2,1)S(1)}, u32[]{:S(2)}, u32[]{:S(2)}) async-start(bf16[8,2,2048]{2,1,0:T(2,128)(2,1)} %reshape.237), calls=%async_computation.3 | async-start | bytes 131072 | tf_op jit(solution)/shard_map/all_to_all | solution.py:26
  65.7 29.2 %all-to-all-start.2 = ((bf16[8,12,4096]{2,1,0:T(8,128)(2,1)}), bf16[8,12,4096]{2,1,0:T(8,128)(2,1)S(1)}, u32[]{:S(2)}, u32[]{:S(2)}) async-start(bf16[8,12,4096]{2,1,0:T(8,128)(2,1)} %broadcast_in_dim.98), calls=%async_computation.2 | async-start | bytes 2097152 | tf_op jit(solution)/shard_map/all_to_all | solution.py:26
  69.3 45.2 %collective-permute-start.1 = (bf16[256,4096]{1,0:T(8,128)(2,1)}, bf16[256,4096]{1,0:T(8,128)(2,1)}, u32[]{:S(2)}, u32[]{:S(2)}) collective-permute-start(bf16[256,4096]{1,0:T(8,128)(2,1)} %param.14), channel_id=1, source_target_pairs={{0,2},{2,0},{1,3},{3,1},{4,6},{6,4},{5,7},{7,5},{8,10},{10,8},{9,1... | collective-permute-start | bytes 6291464 | tf_op jit(solution)/shard_map/ppermute | solution.py:32
  95.9 30.8 %all-to-all-start.4 = ((bf16[12,8,4096]{2,1,0:T(8,128)(2,1)}), bf16[12,8,4096]{2,1,0:T(8,128)(2,1)S(1)}, u32[]{:S(2)}, u32[]{:S(2)}) async-start(bf16[12,8,4096]{2,1,0:T(8,128)(2,1)} %broadcast_in_dim.102), calls=%async_computation.4 | async-start | bytes 1572864 | tf_op jit(solution)/shard_map/all_to_all | solution.py:26
  99.6 32.2 %collective-permute-start = (bf16[256,4096]{1,0:T(8,128)(2,1)}, bf16[256,4096]{1,0:T(8,128)(2,1)}, u32[]{:S(2)}, u32[]{:S(2)}) collective-permute-start(bf16[256,4096]{1,0:T(8,128)(2,1)} %param.14), channel_id=1, source_target_pairs={{0,1},{1,0},{2,3},{3,2},{4,5},{5,4},{6,7},{7,6},{8,9},{9,8},{10,11... | collective-permute-start | bytes 6291464 | tf_op jit(solution)/shard_map/ppermute | solution.py:32
  114.5 19.8 %collective-permute-start.2 = (bf16[256,4096]{1,0:T(8,128)(2,1)}, bf16[256,4096]{1,0:T(8,128)(2,1)}, u32[]{:S(2)}, u32[]{:S(2)}) collective-permute-start(bf16[256,4096]{1,0:T(8,128)(2,1)} %collective-permute-done.1), channel_id=1, source_target_pairs={{0,1},{1,0},{2,3},{3,2},{4,5},{5,4},{6,7},{7,6},{8,9},{9,8},{10,11... | collective-permute-start | bytes 6291464 | tf_op jit(solution)/shard_map/ppermute | solution.py:32
  157.4 13.8 %all-to-all-start.7 = ((f32[32,2,2,192]{3,2,1,0:T(2,128)}), f32[32,2,2,192]{3,2,1,0:T(2,128)S(1)}, u32[]{:S(2)}, u32[]{:S(2)}) async-start(f32[32,2,2,192]{3,2,1,0:T(2,128)} %broadcast_in_dim.105), calls=%async_computation.7 | async-start | bytes 262144 | tf_op jit(solution)/shard_map/all_to_all | solution.py:26
  171.2 16.2 %all-to-all-start.5 = ((f32[4,192,256]{2,1,0:T(8,128)}), f32[4,192,256]{2,1,0:T(8,128)S(1)}, u32[]{:S(2)}, u32[]{:S(2)}) async-start(f32[4,192,256]{2,1,0:T(8,128)} %pad_maximum_fusion.1), calls=%async_computation.5 | async-start | bytes 1572864 | tf_op jit(solution)/shard_map/all_to_all | solution.py:130

commit v2 on v1

--- a/solution.py
+++ b/solution.py
@@ -1,18 +1,20 @@
-import functools
 import math
 
 import jax
 import jax.numpy as jnp
 from jax import lax
+from jax.experimental import pallas as pl
+from jax.experimental.pallas import tpu as pltpu
 from jax.sharding import Mesh
 from jax.sharding import PartitionSpec as P
 
+
 HEAD_DIM = 128
 SEQ = 16
-XH, Y, Z, XL, C = "corpus_0", "corpus_1", "corpus_2", "tensor_0", "tensor_1"
+XH, YH, YL, ZH, ZL, XL, C = "xh", "yh", "yl", "zh", "zl", "xl", "c"
 TENSOR = (XL, C)
-CORPUS = (XH, Y, Z)
-CORPUS_TENSOR = (XH, Y, Z, XL, C)
+CORPUS = (XH, YH, YL, ZH, ZL)
+CORPUS_TENSOR = (*CORPUS, *TENSOR)
 
 score_scale = 50.0
 
@@ -65,12 +67,61 @@
     return jnp.squeeze(peak, axes), total
 
 
-def on_device(q_states, k_states, v_states, residual, out_weight, final_gain, passages, lengths):
-    xh, y, z, xl, c = (lax.axis_size(axis) for axis in CORPUS_TENSOR)
+def score_kernel(rows_ref, *refs):
+    blocks, outs, (stats_ref, held, arrived) = refs[:4], refs[4:8], refs[8:]
+    copies = [
+        pltpu.make_async_copy(block, held.at[i], arrived.at[i]) for i, block in enumerate(blocks)
+    ]
+    for copy in copies:
+        copy.start()
+    count = rows_ref.shape[0]
+    peak = None
+    for i, out in enumerate(outs):
+        copies[i].wait()
+        scores = (
+            lax.dot_general(
+                rows_ref[...], held[i], (((1,), (1,)), ((), ())), preferred_element_type=jnp.float32
+            )
+            * score_scale
+        )
+        out[...] = scores
+        top = jnp.max(scores, axis=1, keepdims=True)
+        peak = top if peak is None else jnp.maximum(peak, top)
+    total = sum(jnp.sum(jnp.exp(out[...] - peak), axis=1, keepdims=True) for out in outs)
+    lane = lax.broadcasted_iota(jnp.int32, (count, 128), 1)
+    both = jnp.where(lane == 0, peak, total)
+    stats_ref[...] = jnp.transpose(both)[: stats_ref.shape[0]]
+
+
+def score_blocks(rows, blocks):
+    count, width = rows.shape
+    passages = blocks[0].shape[0]
+    space = pl.BlockSpec(memory_space=pltpu.VMEM)
+    return pl.pallas_call(
+        score_kernel,
+        name="score_blocks",
+        out_shape=[jax.ShapeDtypeStruct((count, passages), jnp.float32)] * 4
+        + [jax.ShapeDtypeStruct((2, count), jnp.float32)],
+        in_specs=[space] + [pl.BlockSpec(memory_space=pl.ANY)] * 4,
+        out_specs=[space] * 5,
+        scratch_shapes=[
+            pltpu.VMEM((4, passages, width), jnp.bfloat16),
+            pltpu.SemaphoreType.DMA((4,)),
+        ],
+        cost_estimate=pl.CostEstimate(
+            flops=8 * count * passages * width,
+            bytes_accessed=8 * passages * width,
+            transcendentals=4 * count * passages,
+        ),
+    )(rows, *blocks)
+
+
+def step(q_states, k_states, v_states, residual, out_weight, final_gain, passages, lengths):
+    xh, yh, yl, zh, zl, xl, c = (lax.axis_size(axis) for axis in CORPUS_TENSOR)
     tensor = xl * c
     query_count = lengths.shape[0]
     width = out_weight.shape[1]
-    rows = y * z
+    rows = yh * yl * zh * zl * xh
     places = lax.broadcasted_iota(jnp.int32, (query_count, SEQ), 1)
     picker = (places == (lengths - 1)[:, None]).astype(jnp.float32)
     key_rows = k_states.reshape(query_count, SEQ, -1)
@@ -97,55 +148,44 @@
     held, embed = lax.optimization_barrier((passages, embed))
     across = swap(held, XL)
     partner = swap(held, C)
-    across_partner = swap(across, C)
-
-    one_z = to_all(embed[0:1], (Z,))
-    two_y = to_all(embed[1:2], (Y,))
-    one = to_all(one_z.reshape(z, width), (Y,)).reshape(rows, width)
-    two = to_all(two_y.reshape(y, width), (Z,)).reshape(rows, width)
-    gathered = jnp.concatenate([one, two], axis=0)
-
-    def score(block):
-        return (
-            lax.dot_general(
-                gathered, block, (((1,), (1,)), ((), ())), preferred_element_type=jnp.float32
-            )
-            * score_scale
-        )
-
-    blocks = [[score(held), score(partner)], [score(across), score(across_partner)]]
-    local_peak = functools.reduce(
-        jnp.maximum, [jnp.max(s, axis=1) for pair in blocks for s in pair]
-    )
-    local_total = sum(
-        jnp.sum(jnp.exp(s - local_peak[:, None]), axis=1) for pair in blocks for s in pair
-    )
+    both = swap(across, C)
+
+    gathered = to_all(embed, (YH, ZH)).reshape(-1, width)
+    gathered = to_all(gathered, (YL, ZL)).reshape(-1, width)
+
+    *blocks, stats = score_blocks(gathered, (held, partner, across, both))
+
+    own, for_partner, for_across, for_both = blocks
+    from_partner = swap(for_partner, C)
+    from_across = swap(for_across, XL)
+    from_both = lax.ppermute(for_both, TENSOR, [(i, tensor - 1 - i) for i in range(tensor)])
+
+    pairs = to_all(stats, (ZH, ZL, C))
+    pairs = pairs.reshape(zh * zl, c, 2, rows)
+    peak, total = merge(pairs[:, :, 0], pairs[:, :, 1], 0)
+    pairs = to_all(jnp.stack([peak, total]), (XH, YH, YL, XL))
+    pairs = pairs.reshape(xh * yh * yl, xl, 2, c, rows)
+    peak, total = merge(pairs[:, :, 0], pairs[:, :, 1], 0)
+    log_norm = (peak + jnp.log(total)).reshape(tensor, rows)
 
     me_xl, me_c = lax.axis_index(XL), lax.axis_index(C)
-    outgoing = []
-    for a in range(2):
-        for b in range(2):
-            pair = [jnp.where(me_c == b, p[0], p[1]) for p in blocks]
-            outgoing.append(jnp.where(me_xl == a, pair[0], pair[1]))
-    returned = lax.all_to_all(jnp.stack(outgoing), TENSOR, 0, 0, tiled=True)
-
-    pairs = to_all(jnp.stack([local_peak, local_total]), (Z, C)).reshape(z, c, 2, xh * rows)
-    peak, total = merge(pairs[:, :, 0], pairs[:, :, 1], 0)
-    pairs = to_all(jnp.stack([peak, total]), (XH, Y, XL)).reshape(xh * y, xl, 2, c, xh * rows)
-    peak, total = merge(pairs[:, :, 0], pairs[:, :, 1], 0)
-    log_norm = (peak + jnp.log(total)).reshape(tensor, xh * rows)
+    here = [jnp.where(me_c == i, own, from_partner) for i in range(2)]
+    there = [jnp.where(me_c == i, from_across, from_both) for i in range(2)]
+    returned = jnp.stack(
+        [jnp.where(me_xl == i // 2, here[i % 2], there[i % 2]) for i in range(tensor)]
+    )
 
     def ordered(values):
         tail = values.shape[2:]
-        one = values[:, :rows].reshape(tensor, y, z, *tail)
-        two = values[:, rows:].reshape(tensor, z, y, *tail).swapaxes(1, 2)
-        return jnp.moveaxis(jnp.stack([one, two]), 1, 3).reshape(xh * rows * tensor, *tail)
+        values = values.reshape(tensor, yl, zl, yh, zh, xh, *tail)
+        last = tuple(range(6, 6 + len(tail)))
+        return values.transpose((5, 3, 1, 4, 2, 0, *last)).reshape(rows * tensor, *tail)
 
     return ordered(returned), ordered(log_norm)
 
 
 def solution(mesh):
-    split = Mesh(mesh.devices.reshape(2, 8, 12, 2, 2), CORPUS_TENSOR)
+    split = Mesh(mesh.devices.reshape(2, 4, 2, 6, 2, 2, 2), CORPUS_TENSOR)
     in_specs = (
         P(CORPUS, TENSOR),
         P(CORPUS, TENSOR),
@@ -157,6 +197,4 @@
         P(CORPUS),
     )
     out_specs = (P(None, CORPUS_TENSOR), P())
-    return jax.shard_map(
-        on_device, mesh=split, in_specs=in_specs, out_specs=out_specs, check_vma=False
-    )
+    return jax.shard_map(step, mesh=split, in_specs=in_specs, out_specs=out_specs, check_vma=False)

time: 190 us -> 153 us (0.81)
  waiting for transfers between devices: 70.9 us -> 44 us
  blocking collectives: 37.5 us -> 18.1 us
  matrix products: 15.1 us -> 5.01 us
  starting transfers between devices: 46.1 us -> 56 us
  Pallas kernels: 0 us -> 9.23 us
  other arithmetic: 8.53 us -> 6.21 us
  local copies, waits for them, and re-layouts: 10.2 us -> 12.5 us
    all_to_all x5 -> x4, waiting for transfers between devices: 52.6 us -> 23.6 us  [to_all(): lax.all_to_all(jnp.broadcast_to(shard[None], (length, *shard.shape)), axe...]
    all_to_all x2 -> x1, blocking collectives: 37.5 us -> 18.1 us  [step(): terms = lax.all_to_all(terms, (XH, XL, C), 0, 0, tiled=True)]
    all_to_all x5 -> x4, starting transfers between devices: 25.5 us -> 37 us  [to_all(): lax.all_to_all(jnp.broadcast_to(shard[None], (length, *shard.shape)), axe...]
    ppermute x3 -> x5, waiting for transfers between devices: 9 us -> 20.4 us  [swap(): return lax.ppermute(array, axis, [(0, 1), (1, 0)])]
    dot_general x5 -> x1, matrix products: 14.7 us -> 4.58 us  [step(): jnp.dot(context, out_weight, preferred_element_type=jnp.float32)]
    all_to_all x1 -> x0, waiting for transfers between devices: 9.25 us -> none  [on_device(): returned = lax.all_to_all(jnp.stack(outgoing), TENSOR, 0, 0, tiled=True)]
    pallas_call x0 -> x1, Pallas kernels: none -> 9.23 us  [score_blocks(): pl.pallas_call(score_kernel, name='score_blocks', out_shape=[jax.ShapeDty...]
    all_to_all x1 -> x0, starting transfers between devices: 5.57 us -> none  [on_device(): returned = lax.all_to_all(jnp.stack(outgoing), TENSOR, 0, 0, tiled=True)]
  transfers between devices with their start and end apart: 9 -> 10, of which waited for: 7 -> 5; matrix products, arithmetic and copies ran while one was open for 7% -> 4% of each run, Pallas kernels for 0% -> 0%
where the time goes in v2:
time: 153 us; the launch traced here: 152 us
  starting transfers between devices  56 us (37%)
  waiting for transfers between devices  44 us (29%)
  blocking collectives  18.1 us (12%)
  local copies, waits for them, and re-layouts  12.5 us (8%)
  Pallas kernels  9.23 us (6%)
  other arithmetic  6.21 us (4%)
  matrix products  5.01 us (3%)
    all_to_all x4, starting transfers between devices, to_all(): lax.all_to_all(jnp.broadcast_to(shard[None], (length, *shard.shape)), axe...  37 us
    all_to_all x4, waiting for transfers between devices, to_all(): lax.all_to_all(jnp.broadcast_to(shard[None], (length, *shard.shape)), axe...  23.6 us
    ppermute x5, waiting for transfers between devices, swap(): return lax.ppermute(array, axis, [(0, 1), (1, 0)])  20.4 us
    all_to_all x1, blocking collectives, step(): terms = lax.all_to_all(terms, (XH, XL, C), 0, 0, tiled=True)  18.1 us
    ppermute x5, starting transfers between devices, swap(): return lax.ppermute(array, axis, [(0, 1), (1, 0)])  15.4 us
    pallas_call x1, Pallas kernels, score_blocks(): pl.pallas_call(score_kernel, name='score_blocks', out_shape=[jax.ShapeDty...  9.23 us
    dot_general x1, matrix products, step(): jnp.dot(context, out_weight, preferred_element_type=jnp.float32)  4.58 us
    broadcast_in_dim x5, local copies, waits for them, and re-layouts, to_all(): jnp.broadcast_to(shard[None], (length, *shard.shape))  4.54 us
  transfers between devices with their start and end apart: 10, of which 5 were waited for; matrix products, arithmetic and copies ran while one was open for 4% of the time, Pallas kernels for 0%

profile of v2, /device:TPU:1, one launch (start us, length us, event | category | flops | bytes accessed | tf_op | source)
XLA Modules:
  0.0 151.9 jit_solution(5490763180030450279)
XLA Ops:
  0.6 0.8 reshape_reshape.8
  1.4 0.7 broadcast_add_fusion
  2.1 0.7 fusion.20
  2.8 1.0 fusion.5
  3.8 0.8 reshape_reshape.7
  4.6 0.2 fusion.23
  4.8 0.2 fusion.15
  5.0 0.2 fusion.1
  5.2 1.3 fusion.4
  6.6 4.6 %convolution_add_fusion = f32[4,4096]{1,0:T(4,128)S(1)} fusion(bf16[4,1024]{1,0:T(4,128)(2,1)S(1)} %convert_element_type.58, bf16[1024,4096]{1,0:T(8,128)(2,1)} %param.12, f32[4,4096]{1,0:T(4,128)S(1)} %fusion.4, pred[]{:T(512)S(6)} %eq.32), kind=kOutput, calls=%fused_computation | convolution fusion | flops 33587200 | bytes 8527873 | tf_op jit(solution)/shard_map/dot_general | solution.py:136
  11.2 0.2 all_to_all.18
  11.4 18.1 %all_to_all.29 = f32[8,1,4096]{2,1,0:T(1,128)S(1)} all-to-all(f32[8,1,4096]{2,1,0:T(1,128)S(1)} %all_to_all.18), channel_id=1, replica_groups=mesh['xh'=2,'yh'=4,'yl'=2,'zh'=6,'zl'=2,'xl'=2,'c'=2] {'xh','xl','c'}, dimensions={0} | all-to-all | bytes 262144 | tf_op jit(solution)/shard_map/all_to_all | solution.py:144
  29.5 0.3 reduce.4
  30.0 0.1 multiply_reduce_fusion
  30.2 1.1 broadcast_in_dim.74
  31.3 12.5 %all-to-all-start.1 = ((bf16[24,2,4096]{2,1,0:T(2,128)(2,1)}), bf16[24,2,4096]{2,1,0:T(2,128)(2,1)S(1)}, u32[]{:S(2)}, u32[]{:S(2)}) async-start(bf16[24,2,4096]{2,1,0:T(2,128)(2,1)} %broadcast_in_dim.74), calls=%async_computation.1 | async-start | bytes 786432 | tf_op jit(solution)/shard_map/all_to_all | solution.py:28
  43.8 2.2 %collective-permute-start.1 = (bf16[256,4096]{1,0:T(8,128)(2,1)}, bf16[256,4096]{1,0:T(8,128)(2,1)}, u32[]{:S(2)}, u32[]{:S(2)}) collective-permute-start(bf16[256,4096]{1,0:T(8,128)(2,1)} %refs_0_), channel_id=1, source_target_pairs={{0,2},{2,0},{1,3},{3,1},{4,6},{6,4},{5,7},{7,5},{8,10},{10,8},{9,1... | collective-permute-start | bytes 6291464 | tf_op jit(solution)/shard_map/ppermute | solution.py:34
  46.0 15.0 %all-to-all-done.1 = bf16[24,2,4096]{2,1,0:T(2,128)(2,1)S(1)} async-done(((bf16[24,2,4096]{2,1,0:T(2,128)(2,1)}), bf16[24,2,4096]{2,1,0:T(2,128)(2,1)S(1)}, u32[]{:S(2)}, u32[]{:S(2)}) %all-to-all-start.1) | async-done | bytes 393248 | tf_op jit(solution)/shard_map/all_to_all | solution.py:28
  61.0 0.1 broadcast_in_dim.75
  61.2 1.3 broadcast_in_dim.76
  62.5 6.9 %all-to-all-start.2 = ((bf16[4,48,4096]{2,1,0:T(8,128)(2,1)}), bf16[4,48,4096]{2,1,0:T(8,128)(2,1)S(1)}, u32[]{:S(2)}, u32[]{:S(2)}) async-start(bf16[4,48,4096]{2,1,0:T(8,128)(2,1)} %broadcast_in_dim.76), calls=%async_computation.2 | async-start | bytes 3145728 | tf_op jit(solution)/shard_map/all_to_all | solution.py:28
  69.4 5.0 %collective-permute-start = (bf16[256,4096]{1,0:T(8,128)(2,1)}, bf16[256,4096]{1,0:T(8,128)(2,1)S(1)}, u32[]{:S(2)}, u32[]{:S(2)}) collective-permute-start(bf16[256,4096]{1,0:T(8,128)(2,1)} %refs_0_), channel_id=1, source_target_pairs={{0,1},{1,0},{2,3},{3,2},{4,5},{5,4},{6,7},{7,6},{8,9},{9,8},{10,11... | collective-permute-start | bytes 6291464 | tf_op jit(solution)/shard_map/ppermute | solution.py:34
  74.5 17.6 %collective-permute-done.1.refs_2_ = bf16[256,4096]{1,0:T(8,128)(2,1)} collective-permute-done((bf16[256,4096]{1,0:T(8,128)(2,1)}, bf16[256,4096]{1,0:T(8,128)(2,1)}, u32[]{:S(2)}, u32[]{:S(2)}) %collective-permute-start.1) | collective-permute-done | bytes 2097184 | tf_op jit(solution)/shard_map/ppermute | solution.py:34
  92.0 3.9 %collective-permute-start.2 = (bf16[256,4096]{1,0:T(8,128)(2,1)}, bf16[256,4096]{1,0:T(8,128)(2,1)}, u32[]{:S(2)}, u32[]{:S(2)}) collective-permute-start(bf16[256,4096]{1,0:T(8,128)(2,1)} %collective-permute-done.1.refs_2_), channel_id=1, source_target_pairs={{0,1},{1,0},{2,3},{3,2},{4,5},{5,4},{6,7},{7,6},{8,9},{9,8},{10,11... | collective-permute-start | bytes 6291464 | tf_op jit(solution)/shard_map/ppermute | solution.py:34
  96.0 1.3 copy-done.1
  97.2 2.8 %collective-permute-done.2.refs_3_ = bf16[256,4096]{1,0:T(8,128)(2,1)} collective-permute-done((bf16[256,4096]{1,0:T(8,128)(2,1)}, bf16[256,4096]{1,0:T(8,128)(2,1)}, u32[]{:S(2)}, u32[]{:S(2)}) %collective-permute-start.2) | collective-permute-done | bytes 2097184 | tf_op jit(solution)/shard_map/ppermute | solution.py:34
  100.0 1.1 copy-done
  101.2 9.2 %score_blocks.1 = (f32[192,256]{1,0:T(8,128)}, f32[192,256]{1,0:T(8,128)}, f32[192,256]{1,0:T(8,128)}, f32[192,256]{1,0:T(8,128)}, f32[2,192]{1,0:T(2,128)}) custom-call(bf16[192,4096]{1,0:T(8,128)(2,1)} %bitcast.67, bf16[256,4096]{1,0:T(8,128)(2,1)} %refs_0_, bf16[256,4096]{1,0:T(8,128)(2,1)} %copy-done.1, ...), custom_call_target="tpu_custom_call" | custom-call | flops 1610612736 | bytes 8388608 | tf_op jit(solution)/shard_map/score_blocks/pallas_call | solution.py:100
  110.4 1.3 broadcast_in_dim.77
  111.7 10.2 %all-to-all-start.3 = ((f32[24,2,192]{2,1,0:T(2,128)}), f32[24,2,192]{2,1,0:T(2,128)S(1)}, u32[]{:S(2)}, u32[]{:S(2)}) async-start(f32[24,2,192]{2,1,0:T(2,128)} %broadcast_in_dim.77), calls=%async_computation.3 | async-start | bytes 98304 | tf_op jit(solution)/shard_map/all_to_all | solution.py:28
  122.0 2.1 %collective-permute-start.3 = (f32[192,256]{1,0:T(8,128)}, f32[192,256]{1,0:T(8,128)S(1)}, u32[]{:S(2)}, u32[]{:S(2)}) collective-permute-start(f32[192,256]{1,0:T(8,128)} %get-tuple-element.12), channel_id=1, source_target_pairs={{0,1},{1,0},{2,3},{3,2},{4,5},{5,4},{6,7},{7,6},{8,9},{9,8},{10,11... | collective-permute-start | bytes 589832 | tf_op jit(solution)/shard_map/ppermute | solution.py:34
  124.1 2.2 %collective-permute-start.4 = (f32[192,256]{1,0:T(8,128)}, f32[192,256]{1,0:T(8,128)S(1)}, u32[]{:S(2)}, u32[]{:S(2)}) collective-permute-start(f32[192,256]{1,0:T(8,128)} %get-tuple-element.13), channel_id=1, source_target_pairs={{0,2},{2,0},{1,3},{3,1},{4,6},{6,4},{5,7},{7,5},{8,10},{10,8},{9,1... | collective-permute-start | bytes 589832 | tf_op jit(solution)/shard_map/ppermute | solution.py:34
  126.3 3.6 %collective-permute-start.5 = (f32[192,256]{1,0:T(8,128)}, f32[192,256]{1,0:T(8,128)S(1)}, u32[]{:S(2)}, u32[]{:S(2)}) collective-permute-start(f32[192,256]{1,0:T(8,128)} %get-tuple-element.14), channel_id=1, source_target_pairs={{0,3},{1,2},{2,1},{3,0},{4,7},{5,6},{6,5},{7,4},{8,11},{9,10},{10,... | collective-permute-start | bytes 589832 | tf_op jit(solution)/shard_map/ppermute | solution.py:161
  129.9 2.2 %all-to-all-done.3 = f32[24,2,192]{2,1,0:T(2,128)S(1)} async-done(((f32[24,2,192]{2,1,0:T(2,128)}), f32[24,2,192]{2,1,0:T(2,128)S(1)}, u32[]{:S(2)}, u32[]{:S(2)}) %all-to-all-start.3) | async-done | bytes 36896 | tf_op jit(solution)/shard_map/all_to_all | solution.py:28
  132.1 0.7 broadcast_in_dim.79
  132.8 7.4 %all-to-all-start.4 = ((f32[32,2,2,192]{3,2,1,0:T(2,128)}), f32[32,2,2,192]{3,2,1,0:T(2,128)S(1)}, u32[]{:S(2)}, u32[]{:S(2)}) async-start(f32[32,2,2,192]{3,2,1,0:T(2,128)} %broadcast_in_dim.79), calls=%async_computation.4 | async-start | bytes 262144 | tf_op jit(solution)/shard_map/all_to_all | solution.py:28
  140.2 1.0 broadcast_select_fusion.7
  141.2 0.1 stack.24
  141.3 0.1 stack.23
  141.5 0.1 stack.22
  141.6 0.1 stack.21
  141.7 0.4 maximum_bitcast_fusion
  142.1 0.5 copy.41
  142.6 1.1 reshape.151
  143.7 6.4 %all-to-all-done.4 = f32[32,2,2,192]{3,2,1,0:T(2,128)S(1)} async-done(((f32[32,2,2,192]{3,2,1,0:T(2,128)}), f32[32,2,2,192]{3,2,1,0:T(2,128)S(1)}, u32[]{:S(2)}, u32[]{:S(2)}) %all-to-all-start.4) | async-done | bytes 98336 | tf_op jit(solution)/shard_map/all_to_all | solution.py:28
  150.2 0.1 add.17
  150.4 0.7 copy.47
  151.1 0.8 reshape.154
  (22 shorter events, 0.5 us)
Async XLA Ops:
  6.6 23.4 %copy-start.2 = (f32[4096]{0:T(1024)S(1)}, f32[4096]{0:T(1024)}, u32[]{:S(2)}) copy-start(f32[4096]{0:T(1024)} %param.13) | copy-start | bytes 49156
  31.3 29.7 %all-to-all-start.1 = ((bf16[24,2,4096]{2,1,0:T(2,128)(2,1)}), bf16[24,2,4096]{2,1,0:T(2,128)(2,1)S(1)}, u32[]{:S(2)}, u32[]{:S(2)}) async-start(bf16[24,2,4096]{2,1,0:T(2,128)(2,1)} %broadcast_in_dim.74), calls=%async_computation.1 | async-start | bytes 786432 | tf_op jit(solution)/shard_map/all_to_all | solution.py:28
  43.8 48.3 %collective-permute-start.1 = (bf16[256,4096]{1,0:T(8,128)(2,1)}, bf16[256,4096]{1,0:T(8,128)(2,1)}, u32[]{:S(2)}, u32[]{:S(2)}) collective-permute-start(bf16[256,4096]{1,0:T(8,128)(2,1)} %refs_0_), channel_id=1, source_target_pairs={{0,2},{2,0},{1,3},{3,1},{4,6},{6,4},{5,7},{7,5},{8,10},{10,8},{9,1... | collective-permute-start | bytes 6291464 | tf_op jit(solution)/shard_map/ppermute | solution.py:34
  62.5 37.6 %all-to-all-start.2 = ((bf16[4,48,4096]{2,1,0:T(8,128)(2,1)}), bf16[4,48,4096]{2,1,0:T(8,128)(2,1)S(1)}, u32[]{:S(2)}, u32[]{:S(2)}) async-start(bf16[4,48,4096]{2,1,0:T(8,128)(2,1)} %broadcast_in_dim.76), calls=%async_computation.2 | async-start | bytes 3145728 | tf_op jit(solution)/shard_map/all_to_all | solution.py:28
  69.4 26.5 %collective-permute-start = (bf16[256,4096]{1,0:T(8,128)(2,1)}, bf16[256,4096]{1,0:T(8,128)(2,1)S(1)}, u32[]{:S(2)}, u32[]{:S(2)}) collective-permute-start(bf16[256,4096]{1,0:T(8,128)(2,1)} %refs_0_), channel_id=1, source_target_pairs={{0,1},{1,0},{2,3},{3,2},{4,5},{5,4},{6,7},{7,6},{8,9},{9,8},{10,11... | collective-permute-start | bytes 6291464 | tf_op jit(solution)/shard_map/ppermute | solution.py:34
  92.0 8.0 %collective-permute-start.2 = (bf16[256,4096]{1,0:T(8,128)(2,1)}, bf16[256,4096]{1,0:T(8,128)(2,1)}, u32[]{:S(2)}, u32[]{:S(2)}) collective-permute-start(bf16[256,4096]{1,0:T(8,128)(2,1)} %collective-permute-done.1.refs_2_), channel_id=1, source_target_pairs={{0,1},{1,0},{2,3},{3,2},{4,5},{5,4},{6,7},{7,6},{8,9},{9,8},{10,11... | collective-permute-start | bytes 6291464 | tf_op jit(solution)/shard_map/ppermute | solution.py:34
  95.9 1.3 copy-start.1
  100.0 1.1 copy-start
  111.7 20.3 %all-to-all-start.3 = ((f32[24,2,192]{2,1,0:T(2,128)}), f32[24,2,192]{2,1,0:T(2,128)S(1)}, u32[]{:S(2)}, u32[]{:S(2)}) async-start(f32[24,2,192]{2,1,0:T(2,128)} %broadcast_in_dim.77), calls=%async_computation.3 | async-start | bytes 98304 | tf_op jit(solution)/shard_map/all_to_all | solution.py:28
  122.0 18.2 %collective-permute-start.3 = (f32[192,256]{1,0:T(8,128)}, f32[192,256]{1,0:T(8,128)S(1)}, u32[]{:S(2)}, u32[]{:S(2)}) collective-permute-start(f32[192,256]{1,0:T(8,128)} %get-tuple-element.12), channel_id=1, source_target_pairs={{0,1},{1,0},{2,3},{3,2},{4,5},{5,4},{6,7},{7,6},{8,9},{9,8},{10,11... | collective-permute-start | bytes 589832 | tf_op jit(solution)/shard_map/ppermute | solution.py:34
  124.1 16.1 %collective-permute-start.4 = (f32[192,256]{1,0:T(8,128)}, f32[192,256]{1,0:T(8,128)S(1)}, u32[]{:S(2)}, u32[]{:S(2)}) collective-permute-start(f32[192,256]{1,0:T(8,128)} %get-tuple-element.13), channel_id=1, source_target_pairs={{0,2},{2,0},{1,3},{3,1},{4,6},{6,4},{5,7},{7,5},{8,10},{10,8},{9,1... | collective-permute-start | bytes 589832 | tf_op jit(solution)/shard_map/ppermute | solution.py:34
  126.3 13.9 %collective-permute-start.5 = (f32[192,256]{1,0:T(8,128)}, f32[192,256]{1,0:T(8,128)S(1)}, u32[]{:S(2)}, u32[]{:S(2)}) collective-permute-start(f32[192,256]{1,0:T(8,128)} %get-tuple-element.14), channel_id=1, source_target_pairs={{0,3},{1,2},{2,1},{3,0},{4,7},{5,6},{6,5},{7,4},{8,11},{9,10},{10,... | collective-permute-start | bytes 589832 | tf_op jit(solution)/shard_map/ppermute | solution.py:161
  132.8 17.3 %all-to-all-start.4 = ((f32[32,2,2,192]{3,2,1,0:T(2,128)}), f32[32,2,2,192]{3,2,1,0:T(2,128)S(1)}, u32[]{:S(2)}, u32[]{:S(2)}) async-start(f32[32,2,2,192]{3,2,1,0:T(2,128)} %broadcast_in_dim.79), calls=%async_computation.4 | async-start | bytes 262144 | tf_op jit(solution)/shard_map/all_to_all | solution.py:28

commit v3 on v2

v3 whole, which is shorter than its diff:
```python
import functools
import math

import jax
import jax.numpy as jnp
from jax import lax
from jax.experimental import pallas as pl
from jax.experimental.pallas import tpu as pltpu
from jax.sharding import Mesh
from jax.sharding import PartitionSpec as P


HEAD_DIM = 128
SEQ = 16
XH, YH, YL, ZH, ZL, XL, C = "xh", "yh", "yl", "zh", "zl", "xl", "c"
TENSOR = (XL, C)
CORPUS = (XH, YH, YL, ZH, ZL)
CORPUS_TENSOR = (*CORPUS, *TENSOR)

score_scale = 50.0


def size_of(axes):
    return math.prod(lax.axis_size(axis) for axis in axes)


def to_all(shard, axes):
    length = size_of(axes)
    return lax.all_to_all(
        jnp.broadcast_to(shard[None], (length, *shard.shape)), axes, 0, 0, tiled=True
    )


def swap(array, axis):
    return lax.ppermute(array, axis, [(0, 1), (1, 0)])


def project_kernel(lengths_ref, *refs):
    sources, (out_ref, q_ref, k_ref, v_ref, residual_ref, weight_ref, arrived) = refs[:5], refs[5:]
    chunks = weight_ref.shape[0]
    depth = weight_ref.shape[1]
    copies = [
        pltpu.make_async_copy(source, held, arrived.at[i])
        for i, (source, held) in enumerate(
            zip(sources[:4], (q_ref, k_ref, v_ref, residual_ref), strict=True)
        )
    ] + [
        pltpu.make_async_copy(
            sources[4].at[pl.ds(i * depth, depth)], weight_ref.at[i], arrived.at[4 + i]
        )
        for i in range(chunks)
    ]
    for copy in copies:
        copy.start()
    count = lengths_ref.shape[0]
    tokens = count * SEQ
    pair_heads = k_ref.shape[1] // HEAD_DIM
    shared = q_ref.shape[1] // HEAD_DIM // pair_heads
    rows = shared * count

    def last_of(query):
        place = jnp.zeros_like(query)
        for b in range(count):
            place = jnp.where(query == b, b * SEQ + lengths_ref[b] - 1, place)
        return place

    def one_hot(hit):
        return jnp.where(hit, 1.0, 0.0).astype(jnp.bfloat16)

    row = lax.broadcasted_iota(jnp.int32, (rows, tokens), 0)
    token = lax.broadcasted_iota(jnp.int32, (rows, tokens), 1)
    query = row % count
    last = last_of(query)
    allowed = (token >= query * SEQ) & (token <= last)
    picks = [one_hot((token == last) & (row // count == h)) for h in range(shared)]
    for copy in copies[:3]:
        copy.wait()
    total = out_ref.shape[0]
    slot = lax.broadcasted_iota(jnp.int32, (total, rows), 0)
    source_row = lax.broadcasted_iota(jnp.int32, (total, rows), 1)
    spread = [one_hot(source_row == h * count + slot % count) for h in range(shared)]
    parts = []
    for g in range(pair_heads):
        columns = pl.ds(g * HEAD_DIM, HEAD_DIM)
        queries = sum(
            jnp.dot(
                picks[h],
                q_ref[:, pl.ds((g * shared + h) * HEAD_DIM, HEAD_DIM)],
                preferred_element_type=jnp.float32,
            )
            for h in range(shared)
        ).astype(jnp.bfloat16)
        logits = lax.dot_general(
            queries, k_ref[:, columns], (((1,), (1,)), ((), ())), preferred_element_type=jnp.float32
        ) / math.sqrt(HEAD_DIM)
        logits = jnp.where(allowed, logits, -1e30)
        weights = jnp.where(
            allowed, jnp.exp(logits - jnp.max(logits, axis=1, keepdims=True)), 0.0
        )
        attention = (weights / jnp.sum(weights, axis=1, keepdims=True)).astype(jnp.bfloat16)
        context = jnp.dot(
            attention, v_ref[:, columns], preferred_element_type=jnp.float32
        ).astype(jnp.bfloat16)
        parts += [
            jnp.dot(spread[h], context, preferred_element_type=jnp.float32).astype(jnp.bfloat16)
            for h in range(shared)
        ]
    place = lax.broadcasted_iota(jnp.int32, (total, tokens), 1)
    owner = lax.broadcasted_iota(jnp.int32, (total, tokens), 0) % count
    first = lax.axis_index(XL) + lax.axis_index(C) == 0
    copies[3].wait()
    terms = jnp.dot(
        one_hot((place == last_of(owner)) & first),
        residual_ref[...],
        preferred_element_type=jnp.float32,
    )
    per = depth // HEAD_DIM
    for i in range(chunks):
        part = jnp.concatenate(parts[i * per : (i + 1) * per], axis=1)
        copies[4 + i].wait()
        terms = terms + jnp.dot(part, weight_ref[i], preferred_element_type=jnp.float32)
    out_ref[...] = terms


def project(q_states, k_states, v_states, residual, out_weight, lengths, total):
    depth, width = out_weight.shape
    chunks = 4
    whole = [q_states, k_states, v_states, residual]
    arrays = [pltpu.with_memory_space_constraint(x, pltpu.HBM) for x in (*whole, out_weight)]
    return pl.pallas_call(
        project_kernel,
        name="project",
        out_shape=jax.ShapeDtypeStruct((total, width), jnp.float32),
        in_specs=[pl.BlockSpec(memory_space=pltpu.SMEM)]
        + [pl.BlockSpec(memory_space=pltpu.HBM)] * 5,
        out_specs=pl.BlockSpec(memory_space=pltpu.VMEM),
        scratch_shapes=[pltpu.VMEM(x.shape, x.dtype) for x in whole]
        + [
            pltpu.VMEM((chunks, depth // chunks, width), out_weight.dtype),
            pltpu.SemaphoreType.DMA((4 + chunks,)),
        ],
        compiler_params=pltpu.CompilerParams(vmem_limit_bytes=24 * 1024 * 1024),
    )(lengths, *arrays)


def embed_kernel(terms_ref, gain_ref, out_ref):
    groups = out_ref.shape[1]
    per = terms_ref.shape[0] // groups
    rows = []
    for g in range(groups):
        pooled = terms_ref[g * per]
        for t in range(1, per):
            pooled = pooled + terms_ref[g * per + t]
        scaled = pooled * gain_ref[...]
        magnitude = jnp.maximum(jnp.sqrt(jnp.sum(scaled * scaled, axis=1, keepdims=True)), 1.0)
        rows.append(scaled / magnitude)
    embed = jnp.concatenate(rows, axis=0).astype(jnp.bfloat16)
    for slot in range(out_ref.shape[0]):
        out_ref[slot] = embed


def embed_rows(terms, final_gain, groups, copies):
    width = terms.shape[-1]
    space = pl.BlockSpec(memory_space=pltpu.VMEM)
    return pl.pallas_call(
        embed_kernel,
        name="embed_rows",
        out_shape=jax.ShapeDtypeStruct((copies, groups, width), jnp.bfloat16),
        in_specs=[space] * 2,
        out_specs=space,
        compiler_params=pltpu.CompilerParams(vmem_limit_bytes=8 * 1024 * 1024),
    )(terms, final_gain.reshape(1, width))


def merge(peaks, totals, axes):
    peak = jnp.max(peaks, axis=axes, keepdims=True)
    total = jnp.sum(totals * jnp.exp(peaks - peak), axis=axes)
    return jnp.squeeze(peak, axes), total


def score_kernel(rows_ref, *refs):
    blocks, (kept_ref, crossing_ref, stats_ref, held, arrived) = refs[:4], refs[4:]
    outs = [kept_ref.at[0], kept_ref.at[1], crossing_ref.at[0], crossing_ref.at[1]]
    copies = [
        pltpu.make_async_copy(block, held.at[i], arrived.at[i]) for i, block in enumerate(blocks)
    ]
    for copy in copies:
        copy.start()
    count = rows_ref.shape[0]
    peak = None
    for i, out in enumerate(outs):
        copies[i].wait()
        scores = (
            lax.dot_general(
                rows_ref[...], held[i], (((1,), (1,)), ((), ())), preferred_element_type=jnp.float32
            )
            * score_scale
        )
        out[...] = scores
        top = jnp.max(scores, axis=1, keepdims=True)
        peak = top if peak is None else jnp.maximum(peak, top)
    total = sum(jnp.sum(jnp.exp(out[...] - peak), axis=1, keepdims=True) for out in outs)
    lane = lax.broadcasted_iota(jnp.int32, (count, 128), 1)
    stats = jnp.transpose(jnp.where(lane == 0, peak, total))[:2]
    stats_ref[...] = jnp.broadcast_to(stats[None], stats_ref.shape)


def score_blocks(rows, blocks, copies):
    count, width = rows.shape
    passages = blocks[0].shape[0]
    space = pl.BlockSpec(memory_space=pltpu.VMEM)
    blocks = [pltpu.with_memory_space_constraint(block, pltpu.HBM) for block in blocks]
    return pl.pallas_call(
        score_kernel,
        name="score_blocks",
        out_shape=[jax.ShapeDtypeStruct((2, count, passages), jnp.float32)] * 2
        + [jax.ShapeDtypeStruct((copies, 2, count), jnp.float32)],
        in_specs=[space] + [pl.BlockSpec(memory_space=pltpu.HBM)] * 4,
        out_specs=[space] * 3,
        scratch_shapes=[
            pltpu.VMEM((4, passages, width), jnp.bfloat16),
            pltpu.SemaphoreType.DMA((4,)),
        ],
        cost_estimate=pl.CostEstimate(
            flops=8 * count * passages * width,
            bytes_accessed=8 * passages * width,
            transcendentals=4 * count * passages,
        ),
        compiler_params=pltpu.CompilerParams(vmem_limit_bytes=24 * 1024 * 1024),
    )(rows, *blocks)


def arrange_kernel(sizes, kept_ref, crossed_ref, given_ref, out_ref, by_owner, placed):
    xh, yh, yl, zh, zl, tensor = sizes
    me = lax.axis_index(XL) * 2 + lax.axis_index(C)
    for flip, ref in enumerate(
        (kept_ref.at[0], given_ref.at[0], crossed_ref.at[0], given_ref.at[1])
    ):
        for half in range(placed.shape[0]):
            by_owner[me ^ flip, half] = ref[:, pl.ds(half * 128, 128)]
    for t in range(tensor):
        for near in range(yl * zl):
            y0, z0 = near // zl, near % zl
            for y1 in range(yh):
                for x in range(xh):
                    start = (near * yh + y1) * zh * xh + x
                    to = ((x * yh + y1) * yl + y0) * zh * zl + z0
                    for half in range(placed.shape[0]):
                        placed[half, pl.ds(to * tensor + t, zh, stride=zl * tensor)] = by_owner[
                            t, half, pl.ds(start, zh, stride=xh)
                        ]
    for half in range(placed.shape[0]):
        out_ref[:, pl.ds(half * 128, 128)] = placed[half]


def arrange(kept, crossed, given, sizes):
    _, rows, passages = kept.shape
    tensor = sizes[-1]
    space = pl.BlockSpec(memory_space=pltpu.VMEM)
    return pl.pallas_call(
        functools.partial(arrange_kernel, sizes),
        name="arrange",
        out_shape=jax.ShapeDtypeStruct((rows * tensor, passages), jnp.float32),
        in_specs=[space] * 3,
        out_specs=space,
        scratch_shapes=[
            pltpu.VMEM((tensor, passages // 128, rows, 128), jnp.float32),
            pltpu.VMEM((passages // 128, rows * tensor, 128), jnp.float32),
        ],
        compiler_params=pltpu.CompilerParams(vmem_limit_bytes=8 * 1024 * 1024),
    )(kept, crossed, given)


def step(q_states, k_states, v_states, residual, out_weight, final_gain, passages, lengths):
    xh, yh, yl, zh, zl, xl, c = (lax.axis_size(axis) for axis in CORPUS_TENSOR)
    tensor = xl * c
    width = out_weight.shape[1]
    rows = yh * yl * zh * zl * xh
    terms = project(q_states, k_states, v_states, residual, out_weight, lengths, xh * tensor)

    terms = lax.all_to_all(
        terms.reshape(xh * tensor, 1, width), (XH, XL, C), 0, 0, tiled=True
    )

    across = swap(passages, XL)
    partner = swap(passages, C)
    both = swap(across, C)

    embed = embed_rows(terms, final_gain, xh, yh * zh)
    gathered = lax.all_to_all(embed, (YH, ZH), 0, 0, tiled=True).reshape(-1, width)
    gathered = to_all(gathered, (YL, ZL)).reshape(-1, width)

    kept, crossing, stats = score_blocks(
        gathered, (passages, partner, across, both), zh * zl * c
    )

    crossed = swap(crossing, XL)
    given = swap(jnp.stack([kept[1], crossed[1]]), C)
    scores = arrange(kept, crossed, given, (xh, yh, yl, zh, zl, tensor))

    pairs = lax.all_to_all(stats, (ZH, ZL, C), 0, 0, tiled=True)
    pairs = pairs.reshape(zh * zl, c, 2, rows)
    peak, total = merge(pairs[:, :, 0], pairs[:, :, 1], 0)
    pairs = to_all(jnp.stack([peak, total]), (XH, YH, YL, XL))
    pairs = pairs.reshape(xh * yh * yl, xl, 2, c, rows)
    peak, total = merge(pairs[:, :, 0], pairs[:, :, 1], 0)
    log_norm = (peak + jnp.log(total)).reshape(tensor, rows)

    log_norm = log_norm.reshape(tensor, yl, zl, yh, zh, xh).transpose(5, 3, 1, 4, 2, 0)
    return scores, log_norm.reshape(rows * tensor)


def solution(mesh):
    split = Mesh(mesh.devices.reshape(2, 4, 2, 6, 2, 2, 2), CORPUS_TENSOR)
    in_specs = (
        P(CORPUS, TENSOR),
        P(CORPUS, TENSOR),
        P(CORPUS, TENSOR),
        P(CORPUS, None),
        P(TENSOR, None),
        P(),
        P(CORPUS_TENSOR, None),
        P(CORPUS),
    )
    out_specs = (P(None, CORPUS_TENSOR), P())
    return jax.shard_map(step, mesh=split, in_specs=in_specs, out_specs=out_specs, check_vma=False)
```

time: 153 us -> 144 us (0.941)
  local copies, waits for them, and re-layouts: 12.5 us -> 5.88 us
  waiting for transfers between devices: 44 us -> 50.3 us
  other arithmetic: 6.21 us -> 0.26 us
  Pallas kernels: 9.23 us -> 14.8 us
  matrix products: 5.01 us -> 0 us
  starting transfers between devices: 56 us -> 53.1 us
    all_to_all x0 -> x2, waiting for transfers between devices: none -> 22.9 us  [the longest x1 15 us: step(): lax.all_to_all(embed, (YH, ZH), 0, 0, tiled=True).reshape(-1, width)]
    all_to_all x0 -> x2, starting transfers between devices: none -> 22.7 us  [the longest x1 12.5 us: step(): lax.all_to_all(embed, (YH, ZH), 0, 0, tiled=True).reshape(-1, width)]
    all_to_all x4 -> x2, starting transfers between devices: 37 us -> 14.3 us  [to_all(): lax.all_to_all(jnp.broadcast_to(shard[None], (length, *shard.shape)), axe...]
    all_to_all x4 -> x2, waiting for transfers between devices: 23.6 us -> 7.06 us  [to_all(): lax.all_to_all(jnp.broadcast_to(shard[None], (length, *shard.shape)), axe...]
    pallas_call x0 -> x3, Pallas kernels: none -> 6.97 us  [the longest x1 4.72 us: project(): pl.pallas_call(project_kernel, name='project', out_shape=jax.ShapeDtypeSt...]
    dot_general x3 -> x0, matrix products: 5.01 us -> none  [the longest x1 4.58 us: step(): jnp.dot(context, out_weight, preferred_element_type=jnp.float32)]
    ppermute x1 -> x0, starting transfers between devices: 3.58 us -> none  [step(): lax.ppermute(for_both, TENSOR, [(i, tensor - 1 - i) for i in range(tensor)])]
    reduce_sum x5 -> x0, other arithmetic: 2.78 us -> none  [the longest x1 1.34 us: step(): jnp.sum(picker[:, :, None] * residual.reshape(query_count, SEQ, -1).astyp...]
  transfers between devices with their start and end apart: 10 -> 9, of which waited for: 5 -> 5; matrix products, arithmetic and copies ran while one was open for 4% -> 3% of each run, Pallas kernels for 0% -> 0%
where the time goes in v3:
time: 144 us; the launch traced here: 143 us
  starting transfers between devices  53.1 us (37%)
  waiting for transfers between devices  50.3 us (35%)
  blocking collectives  18.1 us (13%)
  Pallas kernels  14.8 us (10%)
  local copies, waits for them, and re-layouts  5.88 us (4%)
    ppermute x5, waiting for transfers between devices, swap(): return lax.ppermute(array, axis, [(0, 1), (1, 0)])  20.4 us
    all_to_all x1, blocking collectives, step(): lax.all_to_all(terms.reshape(xh * tensor, 1, width), (XH, XL, C), 0, 0, t...  18.1 us
    ppermute x5, starting transfers between devices, swap(): return lax.ppermute(array, axis, [(0, 1), (1, 0)])  16.1 us
    all_to_all x1, waiting for transfers between devices, step(): lax.all_to_all(embed, (YH, ZH), 0, 0, tiled=True).reshape(-1, width)  15 us
    all_to_all x2, starting transfers between devices, to_all(): lax.all_to_all(jnp.broadcast_to(shard[None], (length, *shard.shape)), axe...  14.3 us
    all_to_all x1, starting transfers between devices, step(): lax.all_to_all(embed, (YH, ZH), 0, 0, tiled=True).reshape(-1, width)  12.5 us
    all_to_all x1, starting transfers between devices, step(): pairs = lax.all_to_all(stats, (ZH, ZL, C), 0, 0, tiled=True)  10.2 us
    pallas_call x1, Pallas kernels, score_blocks(): pl.pallas_call(score_kernel, name='score_blocks', out_shape=[jax.ShapeDty...  7.87 us
  transfers between devices with their start and end apart: 9, of which 5 were waited for; matrix products, arithmetic and copies ran while one was open for 3% of the time, Pallas kernels for 0%

profile of v3, /device:TPU:1, one launch (start us, length us, event | category | flops | bytes accessed | tf_op | source)
XLA Modules:
  0.0 143.3 jit_solution(4206573293379998704)
XLA Ops:
  0.6 0.0 copy-start
  0.6 0.0 copy-start.1
  0.7 0.7 copy-done.1
  1.3 4.7 %project.1 = f32[8,4096]{1,0:T(8,128)S(1)} custom-call(s32[4]{0:T(128)S(1)} %copy-done.1, bf16[64,1024]{1,0:T(8,128)(2,1)} %refs_0_.2, bf16[64,256]{1,0:T(8,128)(2,1)} %refs_1_.1, bf16[64,256]{1,0:T(8,128)(2,1)} %refs_2_.1, bf16[64,4096]{1,0:T(8,128)(2,1)} %refs_3_.1, bf16[1024,4096]{1,0:T(8,128)(2,1)} %refs_4_.1), custom_call_target="tpu_custom_call" | custom-call | tf_op jit(solution)/shard_map/project/pallas_call | solution.py:130
  6.0 0.1 reshape.30
  6.1 18.1 %all_to_all.25.terms_ref = f32[8,1,4096]{2,1,0:T(1,128)S(1)} all-to-all(f32[8,1,4096]{2,1,0:T(1,128)S(1)} %reshape.30), channel_id=1, replica_groups=mesh['xh'=2,'yh'=4,'yl'=2,'zh'=6,'zl'=2,'xl'=2,'c'=2] {'xh','xl','c'}, dimensions={0} | all-to-all | bytes 262144 | tf_op jit(solution)/shard_map/all_to_all | solution.py:281
  24.2 0.0 copy-done
  24.2 0.9 embed_rows.1
  25.2 12.5 %all-to-all-start.1 = ((bf16[24,2,4096]{2,1,0:T(2,128)(2,1)}), bf16[24,2,4096]{2,1,0:T(2,128)(2,1)S(1)}, u32[]{:S(2)}, u32[]{:S(2)}) async-start(bf16[24,2,4096]{2,1,0:T(2,128)(2,1)} %embed_rows.1), calls=%async_computation.1 | async-start | bytes 786432 | tf_op jit(solution)/shard_map/all_to_all | solution.py:290
  37.6 2.2 %collective-permute-start.1 = (bf16[256,4096]{1,0:T(8,128)(2,1)}, bf16[256,4096]{1,0:T(8,128)(2,1)}, u32[]{:S(2)}, u32[]{:S(2)}) collective-permute-start(bf16[256,4096]{1,0:T(8,128)(2,1)} %refs_0_.3), channel_id=1, source_target_pairs={{0,2},{2,0},{1,3},{3,1},{4,6},{6,4},{5,7},{7,5},{8,10},{10,8},{9,1... | collective-permute-start | bytes 6291464 | tf_op jit(solution)/shard_map/ppermute | solution.py:35
  39.9 15.0 %all-to-all-done.1 = bf16[24,2,4096]{2,1,0:T(2,128)(2,1)S(1)} async-done(((bf16[24,2,4096]{2,1,0:T(2,128)(2,1)}), bf16[24,2,4096]{2,1,0:T(2,128)(2,1)S(1)}, u32[]{:S(2)}, u32[]{:S(2)}) %all-to-all-start.1) | async-done | bytes 393248 | tf_op jit(solution)/shard_map/all_to_all | solution.py:290
  54.9 0.1 broadcast_in_dim.8
  55.1 1.3 broadcast_in_dim.18
  56.4 6.9 %all-to-all-start.2 = ((bf16[4,48,4096]{2,1,0:T(8,128)(2,1)}), bf16[4,48,4096]{2,1,0:T(8,128)(2,1)S(1)}, u32[]{:S(2)}, u32[]{:S(2)}) async-start(bf16[4,48,4096]{2,1,0:T(8,128)(2,1)} %broadcast_in_dim.18), calls=%async_computation.2 | async-start | bytes 3145728 | tf_op jit(solution)/shard_map/all_to_all | solution.py:29
  63.3 5.0 %collective-permute-start = (bf16[256,4096]{1,0:T(8,128)(2,1)}, bf16[256,4096]{1,0:T(8,128)(2,1)S(1)}, u32[]{:S(2)}, u32[]{:S(2)}) collective-permute-start(bf16[256,4096]{1,0:T(8,128)(2,1)} %refs_0_.3), channel_id=1, source_target_pairs={{0,1},{1,0},{2,3},{3,2},{4,5},{5,4},{6,7},{7,6},{8,9},{9,8},{10,11... | collective-permute-start | bytes 6291464 | tf_op jit(solution)/shard_map/ppermute | solution.py:35
  68.3 17.6 %collective-permute-done.1.refs_2_ = bf16[256,4096]{1,0:T(8,128)(2,1)} collective-permute-done((bf16[256,4096]{1,0:T(8,128)(2,1)}, bf16[256,4096]{1,0:T(8,128)(2,1)}, u32[]{:S(2)}, u32[]{:S(2)}) %collective-permute-start.1) | collective-permute-done | bytes 2097184 | tf_op jit(solution)/shard_map/ppermute | solution.py:35
  85.9 3.9 %collective-permute-start.2 = (bf16[256,4096]{1,0:T(8,128)(2,1)}, bf16[256,4096]{1,0:T(8,128)(2,1)}, u32[]{:S(2)}, u32[]{:S(2)}) collective-permute-start(bf16[256,4096]{1,0:T(8,128)(2,1)} %collective-permute-done.1.refs_2_), channel_id=1, source_target_pairs={{0,1},{1,0},{2,3},{3,2},{4,5},{5,4},{6,7},{7,6},{8,9},{9,8},{10,11... | collective-permute-start | bytes 6291464 | tf_op jit(solution)/shard_map/ppermute | solution.py:35
  89.8 0.0 collective-permute-done.refs_1_
  89.8 0.0 copy-start.2
  89.8 1.3 copy-done.2
  91.1 2.8 %collective-permute-done.2.refs_3_ = bf16[256,4096]{1,0:T(8,128)(2,1)} collective-permute-done((bf16[256,4096]{1,0:T(8,128)(2,1)}, bf16[256,4096]{1,0:T(8,128)(2,1)}, u32[]{:S(2)}, u32[]{:S(2)}) %collective-permute-start.2) | collective-permute-done | bytes 2097184 | tf_op jit(solution)/shard_map/ppermute | solution.py:35
  93.9 0.0 all-to-all-done.2
  93.9 7.9 %score_blocks.1 = (f32[2,192,256]{2,1,0:T(8,128)S(1)}, f32[2,192,256]{2,1,0:T(8,128)S(1)}, f32[24,2,192]{2,1,0:T(2,128)}) custom-call(bf16[192,4096]{1,0:T(8,128)(2,1)S(1)} %bitcast.36, bf16[256,4096]{1,0:T(8,128)(2,1)} %refs_0_.3, bf16[256,4096]{1,0:T(8,128)(2,1)} %copy-done.2, bf16[256,4096]{1,0:T(8,128)(2,1)} %collective-permute-done.1.refs_2_, ...), custom_call_target="tpu_custom_call" | custom-call | flops 1610612736 | bytes 8388608 | tf_op jit(solution)/shard_map/score_blocks/pallas_call | solution.py:213
  101.8 10.2 %all-to-all-start.3 = ((f32[24,2,192]{2,1,0:T(2,128)}), f32[24,2,192]{2,1,0:T(2,128)S(1)}, u32[]{:S(2)}, u32[]{:S(2)}) async-start(f32[24,2,192]{2,1,0:T(2,128)} %get-tuple-element.7), calls=%async_computation.3 | async-start | bytes 98304 | tf_op jit(solution)/shard_map/all_to_all | solution.py:301
  112.0 2.2 %collective-permute-start.3 = (f32[2,192,256]{2,1,0:T(8,128)S(1)}, f32[2,192,256]{2,1,0:T(8,128)S(1)}, u32[]{:S(2)}, u32[]{:S(2)}) collective-permute-start(f32[2,192,256]{2,1,0:T(8,128)S(1)} %get-tuple-element.6), channel_id=1, source_target_pairs={{0,2},{2,0},{1,3},{3,1},{4,6},{6,4},{5,7},{7,5},{8,10},{10,8},{9,1... | collective-permute-start | bytes 1179656 | tf_op jit(solution)/shard_map/ppermute | solution.py:35
  114.2 7.8 %all-to-all-done.3 = f32[24,2,192]{2,1,0:T(2,128)S(1)} async-done(((f32[24,2,192]{2,1,0:T(2,128)}), f32[24,2,192]{2,1,0:T(2,128)S(1)}, u32[]{:S(2)}, u32[]{:S(2)}) %all-to-all-start.3) | async-done | bytes 36896 | tf_op jit(solution)/shard_map/all_to_all | solution.py:301
  122.1 0.1 slice_reduce_fusion
  122.2 0.7 broadcast_in_dim.20
  122.9 7.4 %all-to-all-start.4 = ((f32[32,2,2,192]{3,2,1,0:T(2,128)}), f32[32,2,2,192]{3,2,1,0:T(2,128)S(1)}, u32[]{:S(2)}, u32[]{:S(2)}) async-start(f32[32,2,2,192]{3,2,1,0:T(2,128)} %broadcast_in_dim.20), calls=%async_computation.4 | async-start | bytes 262144 | tf_op jit(solution)/shard_map/all_to_all | solution.py:29
  130.3 0.0 collective-permute-done.3.crossed_ref
  130.4 2.8 %collective-permute-start.4 = (f32[2,192,256]{2,1,0:T(8,128)S(1)}, f32[2,192,256]{2,1,0:T(8,128)S(1)}, u32[]{:S(2)}, u32[]{:S(2)}) collective-permute-start(f32[2,192,256]{2,1,0:T(8,128)S(1)} %pad_maximum_fusion), channel_id=1, source_target_pairs={{0,1},{1,0},{2,3},{3,2},{4,5},{5,4},{6,7},{7,6},{8,9},{9,8},{10,11... | collective-permute-start | bytes 1179656 | tf_op jit(solution)/shard_map/ppermute | solution.py:35
  133.2 7.1 %all-to-all-done.4 = f32[32,2,2,192]{3,2,1,0:T(2,128)S(1)} async-done(((f32[32,2,2,192]{3,2,1,0:T(2,128)}), f32[32,2,2,192]{3,2,1,0:T(2,128)S(1)}, u32[]{:S(2)}, u32[]{:S(2)}) %all-to-all-start.4) | async-done | bytes 98336 | tf_op jit(solution)/shard_map/all_to_all | solution.py:29
  140.3 0.1 fusion.1
  140.3 0.1 add.8
  140.5 0.7 copy.22
  141.2 0.8 reshape.35
  142.0 0.0 collective-permute-done.4.given_ref
  142.0 1.3 arrange.1
  (7 shorter events, 0.2 us)
Async XLA Ops:
  0.6 23.6 %copy-start = (f32[4096]{0:T(1024)S(1)}, f32[4096]{0:T(1024)}, u32[]{:S(2)}) copy-start(f32[4096]{0:T(1024)} %param.13) | copy-start | bytes 49156
  0.6 0.7 copy-start.1
  25.2 29.7 %all-to-all-start.1 = ((bf16[24,2,4096]{2,1,0:T(2,128)(2,1)}), bf16[24,2,4096]{2,1,0:T(2,128)(2,1)S(1)}, u32[]{:S(2)}, u32[]{:S(2)}) async-start(bf16[24,2,4096]{2,1,0:T(2,128)(2,1)} %embed_rows.1), calls=%async_computation.1 | async-start | bytes 786432 | tf_op jit(solution)/shard_map/all_to_all | solution.py:290
  37.6 48.3 %collective-permute-start.1 = (bf16[256,4096]{1,0:T(8,128)(2,1)}, bf16[256,4096]{1,0:T(8,128)(2,1)}, u32[]{:S(2)}, u32[]{:S(2)}) collective-permute-start(bf16[256,4096]{1,0:T(8,128)(2,1)} %refs_0_.3), channel_id=1, source_target_pairs={{0,2},{2,0},{1,3},{3,1},{4,6},{6,4},{5,7},{7,5},{8,10},{10,8},{9,1... | collective-permute-start | bytes 6291464 | tf_op jit(solution)/shard_map/ppermute | solution.py:35
  56.4 37.6 %all-to-all-start.2 = ((bf16[4,48,4096]{2,1,0:T(8,128)(2,1)}), bf16[4,48,4096]{2,1,0:T(8,128)(2,1)S(1)}, u32[]{:S(2)}, u32[]{:S(2)}) async-start(bf16[4,48,4096]{2,1,0:T(8,128)(2,1)} %broadcast_in_dim.18), calls=%async_computation.2 | async-start | bytes 3145728 | tf_op jit(solution)/shard_map/all_to_all | solution.py:29
  63.3 26.5 %collective-permute-start = (bf16[256,4096]{1,0:T(8,128)(2,1)}, bf16[256,4096]{1,0:T(8,128)(2,1)S(1)}, u32[]{:S(2)}, u32[]{:S(2)}) collective-permute-start(bf16[256,4096]{1,0:T(8,128)(2,1)} %refs_0_.3), channel_id=1, source_target_pairs={{0,1},{1,0},{2,3},{3,2},{4,5},{5,4},{6,7},{7,6},{8,9},{9,8},{10,11... | collective-permute-start | bytes 6291464 | tf_op jit(solution)/shard_map/ppermute | solution.py:35
  85.9 8.0 %collective-permute-start.2 = (bf16[256,4096]{1,0:T(8,128)(2,1)}, bf16[256,4096]{1,0:T(8,128)(2,1)}, u32[]{:S(2)}, u32[]{:S(2)}) collective-permute-start(bf16[256,4096]{1,0:T(8,128)(2,1)} %collective-permute-done.1.refs_2_), channel_id=1, source_target_pairs={{0,1},{1,0},{2,3},{3,2},{4,5},{5,4},{6,7},{7,6},{8,9},{9,8},{10,11... | collective-permute-start | bytes 6291464 | tf_op jit(solution)/shard_map/ppermute | solution.py:35
  89.8 1.3 copy-start.2
  101.8 20.3 %all-to-all-start.3 = ((f32[24,2,192]{2,1,0:T(2,128)}), f32[24,2,192]{2,1,0:T(2,128)S(1)}, u32[]{:S(2)}, u32[]{:S(2)}) async-start(f32[24,2,192]{2,1,0:T(2,128)} %get-tuple-element.7), calls=%async_computation.3 | async-start | bytes 98304 | tf_op jit(solution)/shard_map/all_to_all | solution.py:301
  112.0 18.3 %collective-permute-start.3 = (f32[2,192,256]{2,1,0:T(8,128)S(1)}, f32[2,192,256]{2,1,0:T(8,128)S(1)}, u32[]{:S(2)}, u32[]{:S(2)}) collective-permute-start(f32[2,192,256]{2,1,0:T(8,128)S(1)} %get-tuple-element.6), channel_id=1, source_target_pairs={{0,2},{2,0},{1,3},{3,1},{4,6},{6,4},{5,7},{7,5},{8,10},{10,8},{9,1... | collective-permute-start | bytes 1179656 | tf_op jit(solution)/shard_map/ppermute | solution.py:35
  122.9 17.3 %all-to-all-start.4 = ((f32[32,2,2,192]{3,2,1,0:T(2,128)}), f32[32,2,2,192]{3,2,1,0:T(2,128)S(1)}, u32[]{:S(2)}, u32[]{:S(2)}) async-start(f32[32,2,2,192]{3,2,1,0:T(2,128)} %broadcast_in_dim.20), calls=%async_computation.4 | async-start | bytes 262144 | tf_op jit(solution)/shard_map/all_to_all | solution.py:29
  130.4 11.6 %collective-permute-start.4 = (f32[2,192,256]{2,1,0:T(8,128)S(1)}, f32[2,192,256]{2,1,0:T(8,128)S(1)}, u32[]{:S(2)}, u32[]{:S(2)}) collective-permute-start(f32[2,192,256]{2,1,0:T(8,128)S(1)} %pad_maximum_fusion), channel_id=1, source_target_pairs={{0,1},{1,0},{2,3},{3,2},{4,5},{5,4},{6,7},{7,6},{8,9},{9,8},{10,11... | collective-permute-start | bytes 1179656 | tf_op jit(solution)/shard_map/ppermute | solution.py:35

commit v4 on v3

--- a/solution.py
+++ b/solution.py
@@ -29,6 +29,14 @@
     return lax.all_to_all(
         jnp.broadcast_to(shard[None], (length, *shard.shape)), axes, 0, 0, tiled=True
     )
+
+
+def shifted(array, axes, along_y, along_z):
+    y, z = size_of(axes[:2]), size_of(axes[2:])
+    moves = [
+        (i * z + j, (i + along_y) % y * z + (j + along_z) % z) for i in range(y) for j in range(z)
+    ]
+    return lax.ppermute(array, axes, moves)
 
 
 def swap(array, axis):
@@ -178,21 +186,21 @@
     return jnp.squeeze(peak, axes), total
 
 
-def score_kernel(rows_ref, *refs):
-    blocks, (kept_ref, crossing_ref, stats_ref, held, arrived) = refs[:4], refs[4:]
+def score_kernel(*refs):
+    parts, blocks, (kept_ref, crossing_ref, stats_ref, rows) = refs[:4], refs[4:8], refs[8:]
     outs = [kept_ref.at[0], kept_ref.at[1], crossing_ref.at[0], crossing_ref.at[1]]
-    copies = [
-        pltpu.make_async_copy(block, held.at[i], arrived.at[i]) for i, block in enumerate(blocks)
-    ]
-    for copy in copies:
-        copy.start()
-    count = rows_ref.shape[0]
+    me = lax.axis_index(YL) * 2 + lax.axis_index(ZL)
+    for flip, part in enumerate(parts):
+        rows[me ^ flip] = part[...]
+    count = rows.shape[0] * rows.shape[1]
     peak = None
-    for i, out in enumerate(outs):
-        copies[i].wait()
+    for block, out in zip(blocks, outs, strict=True):
         scores = (
             lax.dot_general(
-                rows_ref[...], held[i], (((1,), (1,)), ((), ())), preferred_element_type=jnp.float32
+                rows[...].reshape(count, rows.shape[2]),
+                block[...],
+                (((1,), (1,)), ((), ())),
+                preferred_element_type=jnp.float32,
             )
             * score_scale
         )
@@ -205,29 +213,56 @@
     stats_ref[...] = jnp.broadcast_to(stats[None], stats_ref.shape)
 
 
-def score_blocks(rows, blocks, copies):
-    count, width = rows.shape
+def hold_kernel(*refs):
+    count = len(refs) // 2
+    sources, outs, arrived = refs[:count], refs[count : 2 * count], refs[-1]
+    copies = [
+        pltpu.make_async_copy(source, out, arrived.at[i])
+        for i, (source, out) in enumerate(zip(sources, outs, strict=True))
+    ]
+    for copy in copies:
+        copy.start()
+    for copy in copies:
+        copy.wait()
+
+
+def hold(blocks):
+    count = len(blocks)
+    return pl.pallas_call(
+        hold_kernel,
+        name="hold",
+        out_shape=[pltpu.VMEM(block.shape, block.dtype) for block in blocks],
+        in_specs=[pl.BlockSpec(memory_space=pltpu.HBM)] * count,
+        out_specs=[pl.BlockSpec(memory_space=pltpu.VMEM)] * count,
+        scratch_shapes=[pltpu.SemaphoreType.DMA((count,))],
+        cost_estimate=pl.CostEstimate(
+            flops=1, bytes_accessed=4 * sum(b.size for b in blocks), transcendentals=0
+        ),
+        compiler_params=pltpu.CompilerParams(vmem_limit_bytes=12 * 1024 * 1024),
+    )(*[pltpu.with_memory_space_constraint(block, pltpu.HBM) for block in blocks])
+
+
+def score_blocks(parts, blocks, copies):
+    each, width = parts[0].shape
+    count = len(parts) * each
     passages = blocks[0].shape[0]
     space = pl.BlockSpec(memory_space=pltpu.VMEM)
-    blocks = [pltpu.with_memory_space_constraint(block, pltpu.HBM) for block in blocks]
+    blocks = [pltpu.with_memory_space_constraint(block, pltpu.VMEM) for block in blocks]
     return pl.pallas_call(
         score_kernel,
         name="score_blocks",
         out_shape=[jax.ShapeDtypeStruct((2, count, passages), jnp.float32)] * 2
         + [jax.ShapeDtypeStruct((copies, 2, count), jnp.float32)],
-        in_specs=[space] + [pl.BlockSpec(memory_space=pltpu.HBM)] * 4,
+        in_specs=[space] * 8,
         out_specs=[space] * 3,
-        scratch_shapes=[
-            pltpu.VMEM((4, passages, width), jnp.bfloat16),
-            pltpu.SemaphoreType.DMA((4,)),
-        ],
+        scratch_shapes=[pltpu.VMEM((len(parts), each, width), jnp.bfloat16)],
         cost_estimate=pl.CostEstimate(
             flops=8 * count * passages * width,
             bytes_accessed=8 * passages * width,
             transcendentals=4 * count * passages,
         ),
-        compiler_params=pltpu.CompilerParams(vmem_limit_bytes=24 * 1024 * 1024),
-    )(rows, *blocks)
+        compiler_params=pltpu.CompilerParams(vmem_limit_bytes=16 * 1024 * 1024),
+    )(*parts, *blocks)
 
 
 def arrange_kernel(sizes, kept_ref, crossed_ref, given_ref, out_ref, by_owner, placed):
@@ -288,10 +323,15 @@
 
     embed = embed_rows(terms, final_gain, xh, yh * zh)
     gathered = lax.all_to_all(embed, (YH, ZH), 0, 0, tiled=True).reshape(-1, width)
-    gathered = to_all(gathered, (YL, ZL)).reshape(-1, width)
+    shift = functools.partial(shifted, gathered)
+    near_both = shift((YH, YL, ZH, ZL), 1, 1)
+    near_y = shift((YH, YL, ZH, ZL), -1, 0)
+    near_z = shift((YH, YL, ZH, ZL), 0, -1)
+
+    held = hold((passages, partner, across))
 
     kept, crossing, stats = score_blocks(
-        gathered, (passages, partner, across, both), zh * zl * c
+        (gathered, near_z, near_y, near_both), (*held, both), zh * zl * c
     )
 
     crossed = swap(crossing, XL)

time: 144 us -> 172 us (1.19)
  blocking collectives: 18.1 us -> 46.5 us
  starting transfers between devices: 53.1 us -> 55.9 us
  local copies, waits for them, and re-layouts: 5.88 us -> 3.25 us
  Pallas kernels: 14.8 us -> 12.9 us
    all_to_all x0 -> x1, blocking collectives: none -> 36.8 us  [step(): lax.all_to_all(embed, (YH, ZH), 0, 0, tiled=True).reshape(-1, width)]
    all_to_all x1 -> x0, waiting for transfers between devices: 15 us -> none  [step(): lax.all_to_all(embed, (YH, ZH), 0, 0, tiled=True).reshape(-1, width)]
    ppermute x5, starting transfers between devices: 16.1 us -> 30.8 us  [swap(): return lax.ppermute(array, axis, [(0, 1), (1, 0)])]
    ppermute x0 -> x3, starting transfers between devices: none -> 14.4 us  [shifted(): return lax.ppermute(array, axes, moves)]
    all_to_all x1 -> x0, starting transfers between devices: 12.5 us -> none  [step(): lax.all_to_all(embed, (YH, ZH), 0, 0, tiled=True).reshape(-1, width)]
    ppermute x0 -> x3, waiting for transfers between devices: none -> 9.89 us  [shifted(): return lax.ppermute(array, axes, moves)]
    all_to_all x2 -> x1, starting transfers between devices: 14.3 us -> 5.13 us  [to_all(): lax.all_to_all(jnp.broadcast_to(shard[None], (length, *shard.shape)), axe...]
    all_to_all x1, blocking collectives: 18.1 us -> 9.69 us  [step(): lax.all_to_all(terms.reshape(xh * tensor, 1, width), (XH, XL, C), 0, 0, t...]
  transfers between devices with their start and end apart: 9 -> 10, of which waited for: 5 -> 6; matrix products, arithmetic and copies ran while one was open for 3% -> 2% of each run, Pallas kernels for 0% -> 5%
where the time goes in v4:
time: 172 us; the launch traced here: 171 us
  starting transfers between devices  55.9 us (32%)
  waiting for transfers between devices  51.9 us (30%)
  blocking collectives  46.5 us (27%)
  Pallas kernels  12.9 us (8%)
  local copies, waits for them, and re-layouts  3.25 us (2%)
    all_to_all x1, blocking collectives, step(): lax.all_to_all(embed, (YH, ZH), 0, 0, tiled=True).reshape(-1, width)  36.8 us
    ppermute x5, starting transfers between devices, swap(): return lax.ppermute(array, axis, [(0, 1), (1, 0)])  30.8 us
    ppermute x5, waiting for transfers between devices, swap(): return lax.ppermute(array, axis, [(0, 1), (1, 0)])  26.7 us
    ppermute x3, starting transfers between devices, shifted(): return lax.ppermute(array, axes, moves)  14.4 us
    ppermute x3, waiting for transfers between devices, shifted(): return lax.ppermute(array, axes, moves)  9.89 us
    all_to_all x1, blocking collectives, step(): lax.all_to_all(terms.reshape(xh * tensor, 1, width), (XH, XL, C), 0, 0, t...  9.69 us
    all_to_all x1, waiting for transfers between devices, step(): pairs = lax.all_to_all(stats, (ZH, ZL, C), 0, 0, tiled=True)  8.05 us
    all_to_all x1, waiting for transfers between devices, to_all(): lax.all_to_all(jnp.broadcast_to(shard[None], (length, *shard.shape)), axe...  7.22 us
  transfers between devices with their start and end apart: 10, of which 6 were waited for; matrix products, arithmetic and copies ran while one was open for 2% of the time, Pallas kernels for 5%

profile of v4, /device:TPU:1, one launch (start us, length us, event | category | flops | bytes accessed | tf_op | source)
XLA Modules:
  0.0 171.5 jit_solution(2910315453029831709)
XLA Ops:
  0.6 0.0 copy-start
  0.6 3.9 %collective-permute-start.4 = (bf16[256,4096]{1,0:T(8,128)(2,1)}, bf16[256,4096]{1,0:T(8,128)(2,1)}, u32[]{:S(2)}, u32[]{:S(2)}) collective-permute-start(bf16[256,4096]{1,0:T(8,128)(2,1)} %refs_0_.3), channel_id=1, source_target_pairs={{0,2},{2,0},{1,3},{3,1},{4,6},{6,4},{5,7},{7,5},{8,10},{10,8},{9,1... | collective-permute-start | bytes 6291464 | tf_op jit(solution)/shard_map/ppermute | solution.py:43
  4.6 10.4 %collective-permute-start.3 = (bf16[256,4096]{1,0:T(8,128)(2,1)}, bf16[256,4096]{1,0:T(8,128)(2,1)}, u32[]{:S(2)}, u32[]{:S(2)}) collective-permute-start(bf16[256,4096]{1,0:T(8,128)(2,1)} %refs_0_.3), channel_id=1, source_target_pairs={{0,1},{1,0},{2,3},{3,2},{4,5},{5,4},{6,7},{7,6},{8,9},{9,8},{10,11... | collective-permute-start | bytes 6291464 | tf_op jit(solution)/shard_map/ppermute | solution.py:43
  15.0 26.7 %collective-permute-done.4.refs_2_ = bf16[256,4096]{1,0:T(8,128)(2,1)} collective-permute-done((bf16[256,4096]{1,0:T(8,128)(2,1)}, bf16[256,4096]{1,0:T(8,128)(2,1)}, u32[]{:S(2)}, u32[]{:S(2)}) %collective-permute-start.4) | collective-permute-done | bytes 2097184 | tf_op jit(solution)/shard_map/ppermute | solution.py:43
  41.7 11.7 %collective-permute-start.5 = (bf16[256,4096]{1,0:T(8,128)(2,1)}, bf16[256,4096]{1,0:T(8,128)(2,1)S(1)}, u32[]{:S(2)}, u32[]{:S(2)}) collective-permute-start(bf16[256,4096]{1,0:T(8,128)(2,1)} %collective-permute-done.4.refs_2_), channel_id=1, source_target_pairs={{0,1},{1,0},{2,3},{3,2},{4,5},{5,4},{6,7},{7,6},{8,9},{9,8},{10,11... | collective-permute-start | bytes 6291464 | tf_op jit(solution)/shard_map/ppermute | solution.py:43
  53.4 0.0 copy-start.1
  53.4 0.6 copy-done.1
  54.0 4.7 %project.1 = f32[8,4096]{1,0:T(8,128)S(1)} custom-call(s32[4]{0:T(128)S(1)} %copy-done.1, bf16[64,1024]{1,0:T(8,128)(2,1)} %refs_0_.2, bf16[64,256]{1,0:T(8,128)(2,1)} %refs_1_.1, bf16[64,256]{1,0:T(8,128)(2,1)} %refs_2_.1, bf16[64,4096]{1,0:T(8,128)(2,1)} %refs_3_.1, bf16[1024,4096]{1,0:T(8,128)(2,1)} %refs_4_.1), custom_call_target="tpu_custom_call" | custom-call | tf_op jit(solution)/shard_map/project/pallas_call | solution.py:138
  58.8 0.1 reshape.29
  58.9 9.7 %all_to_all.20.terms_ref = f32[8,1,4096]{2,1,0:T(1,128)S(1)} all-to-all(f32[8,1,4096]{2,1,0:T(1,128)S(1)} %reshape.29), channel_id=1, replica_groups=mesh['xh'=2,'yh'=4,'yl'=2,'zh'=6,'zl'=2,'xl'=2,'c'=2] {'xh','xl','c'}, dimensions={0} | all-to-all | bytes 262144 | tf_op jit(solution)/shard_map/all_to_all | solution.py:316
  68.6 0.0 copy-done
  68.6 0.2 embed_rows.1
  68.8 36.8 %all_to_all.21 = bf16[24,2,4096]{2,1,0:T(2,128)(2,1)S(1)} all-to-all(bf16[24,2,4096]{2,1,0:T(2,128)(2,1)S(1)} %embed_rows.1), channel_id=1, replica_groups=mesh['xh'=2,'yh'=4,'yl'=2,'zh'=6,'zl'=2,'xl'=2,'c'=2] {'yh','zh'}, dimensions={0} | all-to-all | bytes 786432 | tf_op jit(solution)/shard_map/all_to_all | solution.py:325
  105.5 0.1 reshape.31.refs_0_
  105.7 10.6 %collective-permute-start = (bf16[48,4096]{1,0:T(8,128)(2,1)S(1)}, bf16[48,4096]{1,0:T(8,128)(2,1)S(1)}, u32[]{:S(2)}, u32[]{:S(2)}) collective-permute-start(bf16[48,4096]{1,0:T(8,128)(2,1)S(1)} %reshape.31.refs_0_), channel_id=1, source_target_pairs={{0,44},{4,0},{8,4},{12,8},{16,12},{20,16},{24,20},{28,24},{32,28},... | collective-permute-start | bytes 1179656 | tf_op jit(solution)/shard_map/ppermute | solution.py:39
  116.2 1.9 %collective-permute-start.1 = (bf16[48,4096]{1,0:T(8,128)(2,1)S(1)}, bf16[48,4096]{1,0:T(8,128)(2,1)S(1)}, u32[]{:S(2)}, u32[]{:S(2)}) collective-permute-start(bf16[48,4096]{1,0:T(8,128)(2,1)S(1)} %reshape.31.refs_0_), channel_id=1, source_target_pairs={{0,336},{4,340},{8,344},{12,348},{16,352},{20,356},{24,360},{28,36... | collective-permute-start | bytes 1179656 | tf_op jit(solution)/shard_map/ppermute | solution.py:39
  118.2 1.9 %collective-permute-start.2 = (bf16[48,4096]{1,0:T(8,128)(2,1)S(1)}, bf16[48,4096]{1,0:T(8,128)(2,1)S(1)}, u32[]{:S(2)}, u32[]{:S(2)}) collective-permute-start(bf16[48,4096]{1,0:T(8,128)(2,1)S(1)} %reshape.31.refs_0_), channel_id=1, source_target_pairs={{0,52},{4,56},{8,60},{12,64},{16,68},{20,72},{24,76},{28,80},{32,8... | collective-permute-start | bytes 1179656 | tf_op jit(solution)/shard_map/ppermute | solution.py:39
  120.1 0.0 collective-permute-done.3.refs_1_
  120.1 2.9 %hold.1 = (bf16[256,4096]{1,0:T(8,128)(2,1)S(1)}, bf16[256,4096]{1,0:T(8,128)(2,1)S(1)}, bf16[256,4096]{1,0:T(8,128)(2,1)S(1)}) custom-call(bf16[256,4096]{1,0:T(8,128)(2,1)} %refs_0_.3, bf16[256,4096]{1,0:T(8,128)(2,1)} %collective-permute-done.3.refs_1_, bf16[256,4096]{1,0:T(8,128)(2,1)} %collective-permute-done.4.refs_2_), custom_call_target="tpu_custom_call" | custom-call | flops 1 | bytes 12582912 | tf_op jit(solution)/shard_map/hold/pallas_call | solution.py:231
  123.0 0.8 collective-permute-done.refs_1_
  123.8 3.8 %collective-permute-done.1.refs_2_ = bf16[48,4096]{1,0:T(8,128)(2,1)S(1)} collective-permute-done((bf16[48,4096]{1,0:T(8,128)(2,1)S(1)}, bf16[48,4096]{1,0:T(8,128)(2,1)S(1)}, u32[]{:S(2)}, u32[]{:S(2)}) %collective-permute-start.1) | collective-permute-done | bytes 393248 | tf_op jit(solution)/shard_map/ppermute | solution.py:39
  127.7 5.2 %collective-permute-done.2.refs_3_ = bf16[48,4096]{1,0:T(8,128)(2,1)S(1)} collective-permute-done((bf16[48,4096]{1,0:T(8,128)(2,1)S(1)}, bf16[48,4096]{1,0:T(8,128)(2,1)S(1)}, u32[]{:S(2)}, u32[]{:S(2)}) %collective-permute-start.2) | collective-permute-done | bytes 393248 | tf_op jit(solution)/shard_map/ppermute | solution.py:39
  132.9 0.0 collective-permute-done.5.refs_7_
  132.9 3.8 %score_blocks.1 = (f32[2,192,256]{2,1,0:T(8,128)S(1)}, f32[2,192,256]{2,1,0:T(8,128)S(1)}, f32[24,2,192]{2,1,0:T(2,128)}) custom-call(bf16[48,4096]{1,0:T(8,128)(2,1)S(1)} %reshape.31.refs_0_, bf16[48,4096]{1,0:T(8,128)(2,1)S(1)} %collective-permute-done.refs_1_, bf16[48,4096]{1,0:T(8,128)(2,1)S(1)} %collective-permute-done.1.refs_2_, ...), custom_call_target="tpu_custom_call" | custom-call | flops 1610612736 | bytes 8388608 | tf_op jit(solution)/shard_map/score_blocks/pallas_call | solution.py:251
  136.7 5.5 %all-to-all-start.2 = ((f32[24,2,192]{2,1,0:T(2,128)}), f32[24,2,192]{2,1,0:T(2,128)S(1)}, u32[]{:S(2)}, u32[]{:S(2)}) async-start(f32[24,2,192]{2,1,0:T(2,128)} %get-tuple-element.13), calls=%async_computation.2 | async-start | bytes 98304 | tf_op jit(solution)/shard_map/all_to_all | solution.py:341
  142.3 2.2 %collective-permute-start.6 = (f32[2,192,256]{2,1,0:T(8,128)S(1)}, f32[2,192,256]{2,1,0:T(8,128)S(1)}, u32[]{:S(2)}, u32[]{:S(2)}) collective-permute-start(f32[2,192,256]{2,1,0:T(8,128)S(1)} %get-tuple-element.12), channel_id=1, source_target_pairs={{0,2},{2,0},{1,3},{3,1},{4,6},{6,4},{5,7},{7,5},{8,10},{10,8},{9,1... | collective-permute-start | bytes 1179656 | tf_op jit(solution)/shard_map/ppermute | solution.py:43
  144.5 8.1 %all-to-all-done.2 = f32[24,2,192]{2,1,0:T(2,128)S(1)} async-done(((f32[24,2,192]{2,1,0:T(2,128)}), f32[24,2,192]{2,1,0:T(2,128)S(1)}, u32[]{:S(2)}, u32[]{:S(2)}) %all-to-all-start.2) | async-done | bytes 36896 | tf_op jit(solution)/shard_map/all_to_all | solution.py:341
  152.5 0.1 slice_reduce_fusion
  152.6 0.7 broadcast_in_dim.5
  153.3 5.1 %all-to-all-start.3 = ((f32[32,2,2,192]{3,2,1,0:T(2,128)}), f32[32,2,2,192]{3,2,1,0:T(2,128)S(1)}, u32[]{:S(2)}, u32[]{:S(2)}) async-start(f32[32,2,2,192]{3,2,1,0:T(2,128)} %broadcast_in_dim.5), calls=%async_computation.3 | async-start | bytes 262144 | tf_op jit(solution)/shard_map/all_to_all | solution.py:29
  158.5 0.0 collective-permute-done.6.crossed_ref
  158.6 2.6 %collective-permute-start.7 = (f32[2,192,256]{2,1,0:T(8,128)S(1)}, f32[2,192,256]{2,1,0:T(8,128)S(1)}, u32[]{:S(2)}, u32[]{:S(2)}) collective-permute-start(f32[2,192,256]{2,1,0:T(8,128)S(1)} %pad_maximum_fusion), channel_id=1, source_target_pairs={{0,1},{1,0},{2,3},{3,2},{4,5},{5,4},{6,7},{7,6},{8,9},{9,8},{10,11... | collective-permute-start | bytes 1179656 | tf_op jit(solution)/shard_map/ppermute | solution.py:43
  161.2 7.2 %all-to-all-done.3 = f32[32,2,2,192]{3,2,1,0:T(2,128)S(1)} async-done(((f32[32,2,2,192]{3,2,1,0:T(2,128)}), f32[32,2,2,192]{3,2,1,0:T(2,128)S(1)}, u32[]{:S(2)}, u32[]{:S(2)}) %all-to-all-start.3) | async-done | bytes 98336 | tf_op jit(solution)/shard_map/all_to_all | solution.py:29
  168.5 0.1 fusion.1
  168.5 0.1 add.8
  168.7 0.7 copy.22
  169.4 0.8 reshape.34
  170.2 0.0 collective-permute-done.7.given_ref
  170.2 1.3 arrange.1
  (7 shorter events, 0.2 us)
Async XLA Ops:
  0.6 67.9 %copy-start = (f32[4096]{0:T(1024)S(1)}, f32[4096]{0:T(1024)}, u32[]{:S(2)}) copy-start(f32[4096]{0:T(1024)} %param.13) | copy-start | bytes 49156
  0.6 41.1 %collective-permute-start.4 = (bf16[256,4096]{1,0:T(8,128)(2,1)}, bf16[256,4096]{1,0:T(8,128)(2,1)}, u32[]{:S(2)}, u32[]{:S(2)}) collective-permute-start(bf16[256,4096]{1,0:T(8,128)(2,1)} %refs_0_.3), channel_id=1, source_target_pairs={{0,2},{2,0},{1,3},{3,1},{4,6},{6,4},{5,7},{7,5},{8,10},{10,8},{9,1... | collective-permute-start | bytes 6291464 | tf_op jit(solution)/shard_map/ppermute | solution.py:43
  4.6 115.5 %collective-permute-start.3 = (bf16[256,4096]{1,0:T(8,128)(2,1)}, bf16[256,4096]{1,0:T(8,128)(2,1)}, u32[]{:S(2)}, u32[]{:S(2)}) collective-permute-start(bf16[256,4096]{1,0:T(8,128)(2,1)} %refs_0_.3), channel_id=1, source_target_pairs={{0,1},{1,0},{2,3},{3,2},{4,5},{5,4},{6,7},{7,6},{8,9},{9,8},{10,11... | collective-permute-start | bytes 6291464 | tf_op jit(solution)/shard_map/ppermute | solution.py:43
  41.7 91.2 %collective-permute-start.5 = (bf16[256,4096]{1,0:T(8,128)(2,1)}, bf16[256,4096]{1,0:T(8,128)(2,1)S(1)}, u32[]{:S(2)}, u32[]{:S(2)}) collective-permute-start(bf16[256,4096]{1,0:T(8,128)(2,1)} %collective-permute-done.4.refs_2_), channel_id=1, source_target_pairs={{0,1},{1,0},{2,3},{3,2},{4,5},{5,4},{6,7},{7,6},{8,9},{9,8},{10,11... | collective-permute-start | bytes 6291464 | tf_op jit(solution)/shard_map/ppermute | solution.py:43
  53.4 0.7 copy-start.1
  105.7 18.1 %collective-permute-start = (bf16[48,4096]{1,0:T(8,128)(2,1)S(1)}, bf16[48,4096]{1,0:T(8,128)(2,1)S(1)}, u32[]{:S(2)}, u32[]{:S(2)}) collective-permute-start(bf16[48,4096]{1,0:T(8,128)(2,1)S(1)} %reshape.31.refs_0_), channel_id=1, source_target_pairs={{0,44},{4,0},{8,4},{12,8},{16,12},{20,16},{24,20},{28,24},{32,28},... | collective-permute-start | bytes 1179656 | tf_op jit(solution)/shard_map/ppermute | solution.py:39
  116.2 11.4 %collective-permute-start.1 = (bf16[48,4096]{1,0:T(8,128)(2,1)S(1)}, bf16[48,4096]{1,0:T(8,128)(2,1)S(1)}, u32[]{:S(2)}, u32[]{:S(2)}) collective-permute-start(bf16[48,4096]{1,0:T(8,128)(2,1)S(1)} %reshape.31.refs_0_), channel_id=1, source_target_pairs={{0,336},{4,340},{8,344},{12,348},{16,352},{20,356},{24,360},{28,36... | collective-permute-start | bytes 1179656 | tf_op jit(solution)/shard_map/ppermute | solution.py:39
  118.2 14.7 %collective-permute-start.2 = (bf16[48,4096]{1,0:T(8,128)(2,1)S(1)}, bf16[48,4096]{1,0:T(8,128)(2,1)S(1)}, u32[]{:S(2)}, u32[]{:S(2)}) collective-permute-start(bf16[48,4096]{1,0:T(8,128)(2,1)S(1)} %reshape.31.refs_0_), channel_id=1, source_target_pairs={{0,52},{4,56},{8,60},{12,64},{16,68},{20,72},{24,76},{28,80},{32,8... | collective-permute-start | bytes 1179656 | tf_op jit(solution)/shard_map/ppermute | solution.py:39
  136.7 15.8 %all-to-all-start.2 = ((f32[24,2,192]{2,1,0:T(2,128)}), f32[24,2,192]{2,1,0:T(2,128)S(1)}, u32[]{:S(2)}, u32[]{:S(2)}) async-start(f32[24,2,192]{2,1,0:T(2,128)} %get-tuple-element.13), calls=%async_computation.2 | async-start | bytes 98304 | tf_op jit(solution)/shard_map/all_to_all | solution.py:341
  142.3 16.2 %collective-permute-start.6 = (f32[2,192,256]{2,1,0:T(8,128)S(1)}, f32[2,192,256]{2,1,0:T(8,128)S(1)}, u32[]{:S(2)}, u32[]{:S(2)}) collective-permute-start(f32[2,192,256]{2,1,0:T(8,128)S(1)} %get-tuple-element.12), channel_id=1, source_target_pairs={{0,2},{2,0},{1,3},{3,1},{4,6},{6,4},{5,7},{7,5},{8,10},{10,8},{9,1... | collective-permute-start | bytes 1179656 | tf_op jit(solution)/shard_map/ppermute | solution.py:43
  153.3 15.1 %all-to-all-start.3 = ((f32[32,2,2,192]{3,2,1,0:T(2,128)}), f32[32,2,2,192]{3,2,1,0:T(2,128)S(1)}, u32[]{:S(2)}, u32[]{:S(2)}) async-start(f32[32,2,2,192]{3,2,1,0:T(2,128)} %broadcast_in_dim.5), calls=%async_computation.3 | async-start | bytes 262144 | tf_op jit(solution)/shard_map/all_to_all | solution.py:29
  158.6 11.6 %collective-permute-start.7 = (f32[2,192,256]{2,1,0:T(8,128)S(1)}, f32[2,192,256]{2,1,0:T(8,128)S(1)}, u32[]{:S(2)}, u32[]{:S(2)}) collective-permute-start(f32[2,192,256]{2,1,0:T(8,128)S(1)} %pad_maximum_fusion), channel_id=1, source_target_pairs={{0,1},{1,0},{2,3},{3,2},{4,5},{5,4},{6,7},{7,6},{8,9},{9,8},{10,11... | collective-permute-start | bytes 1179656 | tf_op jit(solution)/shard_map/ppermute | solution.py:43

commit v5 on v4

--- a/solution.py
+++ b/solution.py
@@ -24,11 +24,40 @@
     return math.prod(lax.axis_size(axis) for axis in axes)
 
 
-def to_all(shard, axes):
-    length = size_of(axes)
-    return lax.all_to_all(
-        jnp.broadcast_to(shard[None], (length, *shard.shape)), axes, 0, 0, tiled=True
-    )
+def finish_kernel(sizes, pairs_ref, out_ref):
+    xh, yh, yl, zh, zl, xl, c = sizes
+    members, count = pairs_ref.shape[0] // xl, pairs_ref.shape[-1]
+    row = lax.broadcasted_iota(jnp.int32, (count, out_ref.shape[0]), 0)
+    x, z1, y1 = row % xh, row // xh % zh, row // (xh * zh) % yh
+    z0, y0 = row // (xh * zh * yh) % zl, row // (xh * zh * yh * zl)
+    place = (((x * yh + y1) * yl + y0) * zh + z1) * zl + z0
+    target = lax.broadcasted_iota(jnp.int32, row.shape, 1)
+    out = jnp.zeros((1, out_ref.shape[0]), jnp.float32)
+    for t in range(xl * c):
+        peak, total = merged([pairs_ref[m * xl + t // c, t % c] for m in range(members)])
+        value = peak + jnp.log(total)
+        high = value.astype(jnp.bfloat16)
+        rest = value - high.astype(jnp.float32)
+        middle = rest.astype(jnp.bfloat16)
+        low = (rest - middle.astype(jnp.float32)).astype(jnp.bfloat16)
+        chosen = jnp.where(place * (xl * c) + t == target, 1.0, 0.0).astype(jnp.bfloat16)
+        for term in (low, middle, high):
+            spread = jnp.broadcast_to(term.astype(jnp.float32), (8, count)).astype(jnp.bfloat16)
+            out = out + jnp.dot(spread, chosen, preferred_element_type=jnp.float32)[:1]
+    out_ref[...] = out[0]
+
+
+def finish(pairs, sizes):
+    space = pl.BlockSpec(memory_space=pltpu.VMEM)
+    queries = pairs.shape[-1] * sizes[-1] * sizes[-2]
+    return pl.pallas_call(
+        functools.partial(finish_kernel, sizes),
+        name="finish",
+        out_shape=jax.ShapeDtypeStruct((queries,), jnp.float32),
+        in_specs=[space],
+        out_specs=space,
+        compiler_params=pltpu.CompilerParams(vmem_limit_bytes=8 * 1024 * 1024),
+    )(pairs)
 
 
 def shifted(array, axes, along_y, along_z):
@@ -43,8 +72,11 @@
     return lax.ppermute(array, axis, [(0, 1), (1, 0)])
 
 
-def project_kernel(lengths_ref, *refs):
-    sources, (out_ref, q_ref, k_ref, v_ref, residual_ref, weight_ref, arrived) = refs[:5], refs[5:]
+def project_kernel(*refs):
+    sources, lengths, refs = refs[:5], refs[5], refs[6:]
+    out_ref, q_ref, k_ref, v_ref, residual_ref, weight_ref, lengths_ref, arrived, known = refs
+    counted = pltpu.make_async_copy(lengths, lengths_ref, known)
+    counted.start()
     chunks = weight_ref.shape[0]
     depth = weight_ref.shape[1]
     copies = [
@@ -60,6 +92,7 @@
     ]
     for copy in copies:
         copy.start()
+    counted.wait()
     count = lengths_ref.shape[0]
     tokens = count * SEQ
     pair_heads = k_ref.shape[1] // HEAD_DIM
@@ -127,28 +160,32 @@
         part = jnp.concatenate(parts[i * per : (i + 1) * per], axis=1)
         copies[4 + i].wait()
         terms = terms + jnp.dot(part, weight_ref[i], preferred_element_type=jnp.float32)
-    out_ref[...] = terms
+    for d in range(total):
+        out_ref[d] = terms[d : d + 1]
 
 
 def project(q_states, k_states, v_states, residual, out_weight, lengths, total):
     depth, width = out_weight.shape
     chunks = 4
     whole = [q_states, k_states, v_states, residual]
-    arrays = [pltpu.with_memory_space_constraint(x, pltpu.HBM) for x in (*whole, out_weight)]
+    arrays = [
+        pltpu.with_memory_space_constraint(x, pltpu.HBM) for x in (*whole, out_weight, lengths)
+    ]
     return pl.pallas_call(
         project_kernel,
         name="project",
-        out_shape=jax.ShapeDtypeStruct((total, width), jnp.float32),
-        in_specs=[pl.BlockSpec(memory_space=pltpu.SMEM)]
-        + [pl.BlockSpec(memory_space=pltpu.HBM)] * 5,
+        out_shape=jax.ShapeDtypeStruct((total, 1, width), jnp.float32),
+        in_specs=[pl.BlockSpec(memory_space=pltpu.HBM)] * 6,
         out_specs=pl.BlockSpec(memory_space=pltpu.VMEM),
         scratch_shapes=[pltpu.VMEM(x.shape, x.dtype) for x in whole]
         + [
             pltpu.VMEM((chunks, depth // chunks, width), out_weight.dtype),
+            pltpu.SMEM(lengths.shape, lengths.dtype),
             pltpu.SemaphoreType.DMA((4 + chunks,)),
+            pltpu.SemaphoreType.DMA,
         ],
         compiler_params=pltpu.CompilerParams(vmem_limit_bytes=24 * 1024 * 1024),
-    )(lengths, *arrays)
+    )(*arrays)
 
 
 def embed_kernel(terms_ref, gain_ref, out_ref):
@@ -180,10 +217,33 @@
     )(terms, final_gain.reshape(1, width))
 
 
-def merge(peaks, totals, axes):
-    peak = jnp.max(peaks, axis=axes, keepdims=True)
-    total = jnp.sum(totals * jnp.exp(peaks - peak), axis=axes)
-    return jnp.squeeze(peak, axes), total
+def merged(rows):
+    peaks = [row[:1] for row in rows]
+    peak = functools.reduce(jnp.maximum, peaks)
+    return peak, sum(row[1:] * jnp.exp(p - peak) for row, p in zip(rows, peaks, strict=True))
+
+
+def merge_kernel(group, pairs_ref, out_ref):
+    members = pairs_ref.shape[0] // group
+    parts = [
+        jnp.concatenate(merged([pairs_ref[m * group + part] for m in range(members)]), axis=0)
+        for part in range(group)
+    ]
+    for slot in range(out_ref.shape[0]):
+        for part in range(group):
+            out_ref[slot, part] = parts[part]
+
+
+def merge(pairs, group, copies):
+    space = pl.BlockSpec(memory_space=pltpu.VMEM)
+    return pl.pallas_call(
+        functools.partial(merge_kernel, group),
+        name="merge",
+        out_shape=jax.ShapeDtypeStruct((copies, group, *pairs.shape[1:]), jnp.float32),
+        in_specs=[space],
+        out_specs=space,
+        compiler_params=pltpu.CompilerParams(vmem_limit_bytes=8 * 1024 * 1024),
+    )(pairs)
 
 
 def score_kernel(*refs):
@@ -310,12 +370,9 @@
     xh, yh, yl, zh, zl, xl, c = (lax.axis_size(axis) for axis in CORPUS_TENSOR)
     tensor = xl * c
     width = out_weight.shape[1]
-    rows = yh * yl * zh * zl * xh
     terms = project(q_states, k_states, v_states, residual, out_weight, lengths, xh * tensor)
 
-    terms = lax.all_to_all(
-        terms.reshape(xh * tensor, 1, width), (XH, XL, C), 0, 0, tiled=True
-    )
+    terms = lax.all_to_all(terms, (XH, XL, C), 0, 0, tiled=True)
 
     across = swap(passages, XL)
     partner = swap(passages, C)
@@ -339,15 +396,8 @@
     scores = arrange(kept, crossed, given, (xh, yh, yl, zh, zl, tensor))
 
     pairs = lax.all_to_all(stats, (ZH, ZL, C), 0, 0, tiled=True)
-    pairs = pairs.reshape(zh * zl, c, 2, rows)
-    peak, total = merge(pairs[:, :, 0], pairs[:, :, 1], 0)
-    pairs = to_all(jnp.stack([peak, total]), (XH, YH, YL, XL))
-    pairs = pairs.reshape(xh * yh * yl, xl, 2, c, rows)
-    peak, total = merge(pairs[:, :, 0], pairs[:, :, 1], 0)
-    log_norm = (peak + jnp.log(total)).reshape(tensor, rows)
-
-    log_norm = log_norm.reshape(tensor, yl, zl, yh, zh, xh).transpose(5, 3, 1, 4, 2, 0)
-    return scores, log_norm.reshape(rows * tensor)
+    pairs = lax.all_to_all(merge(pairs, c, xh * yh * yl * xl), (XH, YH, YL, XL), 0, 0, tiled=True)
+    return scores, finish(pairs, (xh, yh, yl, zh, zl, xl, c))
 
 
 def solution(mesh):

time: 172 us -> 181 us (1.052)
  blocking collectives: 46.5 us -> 74 us
  starting transfers between devices: 55.9 us -> 47.4 us
  waiting for transfers between devices: 51.9 us -> 44.9 us
  local copies, waits for them, and re-layouts: 3.25 us -> 0.18 us
    all_to_all x1 -> x3, blocking collectives: 9.69 us -> 37.3 us  [the longest x1 14.6 us: step(): lax.all_to_all(merge(pairs, c, xh * yh * yl * xl), (XH, YH, YL, XL), 0, 0...]
    all_to_all x2 -> x0, waiting for transfers between devices: 15.3 us -> none  [the longest x1 8.05 us: step(): pairs = lax.all_to_all(stats, (ZH, ZL, C), 0, 0, tiled=True)]
    all_to_all x2 -> x0, starting transfers between devices: 10.7 us -> none  [the longest x1 5.54 us: step(): pairs = lax.all_to_all(stats, (ZH, ZL, C), 0, 0, tiled=True)]
    ppermute x5, waiting for transfers between devices: 26.7 us -> 35.1 us  [swap(): return lax.ppermute(array, axis, [(0, 1), (1, 0)])]
    ppermute x5, starting transfers between devices: 30.8 us -> 33 us  [swap(): return lax.ppermute(array, axis, [(0, 1), (1, 0)])]
  transfers between devices with their start and end apart: 10 -> 8, of which waited for: 6 -> 5; matrix products, arithmetic and copies ran while one was open for 2% -> 0% of each run, Pallas kernels for 5% -> 5%
where the time goes in v5:
time: 181 us
  blocking collectives  74 us (41%)
  starting transfers between devices  47.4 us (26%)
  waiting for transfers between devices  44.9 us (25%)
  Pallas kernels  13.2 us (7%)
    all_to_all x1, blocking collectives, step(): lax.all_to_all(embed, (YH, ZH), 0, 0, tiled=True).reshape(-1, width)  36.8 us
    ppermute x5, waiting for transfers between devices, swap(): return lax.ppermute(array, axis, [(0, 1), (1, 0)])  35.1 us
    ppermute x5, starting transfers between devices, swap(): return lax.ppermute(array, axis, [(0, 1), (1, 0)])  33 us
    all_to_all x1, blocking collectives, step(): lax.all_to_all(merge(pairs, c, xh * yh * yl * xl), (XH, YH, YL, XL), 0, 0...  14.6 us
    ppermute x3, starting transfers between devices, shifted(): return lax.ppermute(array, axes, moves)  14.4 us
    all_to_all x1, blocking collectives, step(): pairs = lax.all_to_all(stats, (ZH, ZL, C), 0, 0, tiled=True)  12.9 us
    ppermute x3, waiting for transfers between devices, shifted(): return lax.ppermute(array, axes, moves)  9.89 us
    all_to_all x1, blocking collectives, step(): terms = lax.all_to_all(terms, (XH, XL, C), 0, 0, tiled=True)  9.69 us
  transfers between devices with their start and end apart: 8, of which 5 were waited for; matrix products, arithmetic and copies ran while one was open for 0% of the time, Pallas kernels for 5%

profile of v5, /device:TPU:1, one launch (start us, length us, event | category | flops | bytes accessed | tf_op | source)
XLA Modules:
  0.0 180.5 jit_solution(4255324436782864423)
XLA Ops:
  0.6 0.0 copy-start
  0.6 3.9 %collective-permute-start.4 = (bf16[256,4096]{1,0:T(8,128)(2,1)}, bf16[256,4096]{1,0:T(8,128)(2,1)}, u32[]{:S(2)}, u32[]{:S(2)}) collective-permute-start(bf16[256,4096]{1,0:T(8,128)(2,1)} %refs_0_.3), channel_id=1, source_target_pairs={{0,2},{2,0},{1,3},{3,1},{4,6},{6,4},{5,7},{7,5},{8,10},{10,8},{9,1... | collective-permute-start | bytes 6291464 | tf_op jit(solution)/shard_map/ppermute | solution.py:72
  4.6 10.4 %collective-permute-start.3 = (bf16[256,4096]{1,0:T(8,128)(2,1)}, bf16[256,4096]{1,0:T(8,128)(2,1)}, u32[]{:S(2)}, u32[]{:S(2)}) collective-permute-start(bf16[256,4096]{1,0:T(8,128)(2,1)} %refs_0_.3), channel_id=1, source_target_pairs={{0,1},{1,0},{2,3},{3,2},{4,5},{5,4},{6,7},{7,6},{8,9},{9,8},{10,11... | collective-permute-start | bytes 6291464 | tf_op jit(solution)/shard_map/ppermute | solution.py:72
  15.0 26.7 %collective-permute-done.4.refs_2_ = bf16[256,4096]{1,0:T(8,128)(2,1)} collective-permute-done((bf16[256,4096]{1,0:T(8,128)(2,1)}, bf16[256,4096]{1,0:T(8,128)(2,1)}, u32[]{:S(2)}, u32[]{:S(2)}) %collective-permute-start.4) | collective-permute-done | bytes 2097184 | tf_op jit(solution)/shard_map/ppermute | solution.py:72
  41.7 11.7 %collective-permute-start.5 = (bf16[256,4096]{1,0:T(8,128)(2,1)}, bf16[256,4096]{1,0:T(8,128)(2,1)S(1)}, u32[]{:S(2)}, u32[]{:S(2)}) collective-permute-start(bf16[256,4096]{1,0:T(8,128)(2,1)} %collective-permute-done.4.refs_2_), channel_id=1, source_target_pairs={{0,1},{1,0},{2,3},{3,2},{4,5},{5,4},{6,7},{7,6},{8,9},{9,8},{10,11... | collective-permute-start | bytes 6291464 | tf_op jit(solution)/shard_map/ppermute | solution.py:72
  53.4 4.2 %project.1 = f32[8,1,4096]{2,1,0:T(1,128)S(1)} custom-call(bf16[64,1024]{1,0:T(8,128)(2,1)} %refs_0_.2, bf16[64,256]{1,0:T(8,128)(2,1)} %refs_1_.1, bf16[64,256]{1,0:T(8,128)(2,1)} %refs_2_.1, bf16[64,4096]{1,0:T(8,128)(2,1)} %refs_3_.1, bf16[1024,4096]{1,0:T(8,128)(2,1)} %refs_4_.1, s32[4]{0:T(128)} %refs_5_.1), custom_call_target="tpu_custom_call" | custom-call | tf_op jit(solution)/shard_map/project/pallas_call | solution.py:174
  57.6 9.7 %all_to_all.20.terms_ref = f32[8,1,4096]{2,1,0:T(1,128)S(1)} all-to-all(f32[8,1,4096]{2,1,0:T(1,128)S(1)} %project.1), channel_id=1, replica_groups=mesh['xh'=2,'yh'=4,'yl'=2,'zh'=6,'zl'=2,'xl'=2,'c'=2] {'xh','xl','c'}, dimensions={0} | all-to-all | bytes 262144 | tf_op jit(solution)/shard_map/all_to_all | solution.py:375
  67.3 0.0 copy-done
  67.3 0.2 embed_rows.1
  67.5 36.8 %all_to_all.21 = bf16[24,2,4096]{2,1,0:T(2,128)(2,1)S(1)} all-to-all(bf16[24,2,4096]{2,1,0:T(2,128)(2,1)S(1)} %embed_rows.1), channel_id=1, replica_groups=mesh['xh'=2,'yh'=4,'yl'=2,'zh'=6,'zl'=2,'xl'=2,'c'=2] {'yh','zh'}, dimensions={0} | all-to-all | bytes 786432 | tf_op jit(solution)/shard_map/all_to_all | solution.py:382
  104.2 0.1 reshape.11.refs_0_
  104.4 10.6 %collective-permute-start = (bf16[48,4096]{1,0:T(8,128)(2,1)S(1)}, bf16[48,4096]{1,0:T(8,128)(2,1)S(1)}, u32[]{:S(2)}, u32[]{:S(2)}) collective-permute-start(bf16[48,4096]{1,0:T(8,128)(2,1)S(1)} %reshape.11.refs_0_), channel_id=1, source_target_pairs={{0,44},{4,0},{8,4},{12,8},{16,12},{20,16},{24,20},{28,24},{32,28},... | collective-permute-start | bytes 1179656 | tf_op jit(solution)/shard_map/ppermute | solution.py:68
  115.0 1.9 %collective-permute-start.1 = (bf16[48,4096]{1,0:T(8,128)(2,1)S(1)}, bf16[48,4096]{1,0:T(8,128)(2,1)S(1)}, u32[]{:S(2)}, u32[]{:S(2)}) collective-permute-start(bf16[48,4096]{1,0:T(8,128)(2,1)S(1)} %reshape.11.refs_0_), channel_id=1, source_target_pairs={{0,336},{4,340},{8,344},{12,348},{16,352},{20,356},{24,360},{28,36... | collective-permute-start | bytes 1179656 | tf_op jit(solution)/shard_map/ppermute | solution.py:68
  116.9 1.9 %collective-permute-start.2 = (bf16[48,4096]{1,0:T(8,128)(2,1)S(1)}, bf16[48,4096]{1,0:T(8,128)(2,1)S(1)}, u32[]{:S(2)}, u32[]{:S(2)}) collective-permute-start(bf16[48,4096]{1,0:T(8,128)(2,1)S(1)} %reshape.11.refs_0_), channel_id=1, source_target_pairs={{0,52},{4,56},{8,60},{12,64},{16,68},{20,72},{24,76},{28,80},{32,8... | collective-permute-start | bytes 1179656 | tf_op jit(solution)/shard_map/ppermute | solution.py:68
  118.8 0.0 collective-permute-done.3.refs_1_
  118.8 2.9 %hold.1 = (bf16[256,4096]{1,0:T(8,128)(2,1)S(1)}, bf16[256,4096]{1,0:T(8,128)(2,1)S(1)}, bf16[256,4096]{1,0:T(8,128)(2,1)S(1)}) custom-call(bf16[256,4096]{1,0:T(8,128)(2,1)} %refs_0_.3, bf16[256,4096]{1,0:T(8,128)(2,1)} %collective-permute-done.3.refs_1_, bf16[256,4096]{1,0:T(8,128)(2,1)} %collective-permute-done.4.refs_2_), custom_call_target="tpu_custom_call" | custom-call | flops 1 | bytes 12582912 | tf_op jit(solution)/shard_map/hold/pallas_call | solution.py:291
  121.7 0.8 collective-permute-done.refs_1_
  122.5 3.8 %collective-permute-done.1.refs_2_ = bf16[48,4096]{1,0:T(8,128)(2,1)S(1)} collective-permute-done((bf16[48,4096]{1,0:T(8,128)(2,1)S(1)}, bf16[48,4096]{1,0:T(8,128)(2,1)S(1)}, u32[]{:S(2)}, u32[]{:S(2)}) %collective-permute-start.1) | collective-permute-done | bytes 393248 | tf_op jit(solution)/shard_map/ppermute | solution.py:68
  126.4 5.2 %collective-permute-done.2.refs_3_ = bf16[48,4096]{1,0:T(8,128)(2,1)S(1)} collective-permute-done((bf16[48,4096]{1,0:T(8,128)(2,1)S(1)}, bf16[48,4096]{1,0:T(8,128)(2,1)S(1)}, u32[]{:S(2)}, u32[]{:S(2)}) %collective-permute-start.2) | collective-permute-done | bytes 393248 | tf_op jit(solution)/shard_map/ppermute | solution.py:68
  131.6 0.0 collective-permute-done.5.refs_7_
  131.6 3.2 %score_blocks.1 = (f32[2,192,256]{2,1,0:T(8,128)S(1)}, f32[2,192,256]{2,1,0:T(8,128)S(1)}, f32[24,2,192]{2,1,0:T(2,128)S(1)}) custom-call(bf16[48,4096]{1,0:T(8,128)(2,1)S(1)} %reshape.11.refs_0_, bf16[48,4096]{1,0:T(8,128)(2,1)S(1)} %collective-permute-done.refs_1_, bf16[48,4096]{1,0:T(8,128)(2,1)S(1)} %collective-permute-done.1.refs_2_, ...), custom_call_target="tpu_custom_call" | custom-call | flops 1610612736 | bytes 8388608 | tf_op jit(solution)/shard_map/score_blocks/pallas_call | solution.py:311
  134.8 2.2 %collective-permute-start.6 = (f32[2,192,256]{2,1,0:T(8,128)S(1)}, f32[2,192,256]{2,1,0:T(8,128)S(1)}, u32[]{:S(2)}, u32[]{:S(2)}) collective-permute-start(f32[2,192,256]{2,1,0:T(8,128)S(1)} %get-tuple-element.12), channel_id=1, source_target_pairs={{0,2},{2,0},{1,3},{3,1},{4,6},{6,4},{5,7},{7,5},{8,10},{10,8},{9,1... | collective-permute-start | bytes 1179656 | tf_op jit(solution)/shard_map/ppermute | solution.py:72
  137.0 8.3 %collective-permute-done.6.crossed_ref = f32[2,192,256]{2,1,0:T(8,128)S(1)} collective-permute-done((f32[2,192,256]{2,1,0:T(8,128)S(1)}, f32[2,192,256]{2,1,0:T(8,128)S(1)}, u32[]{:S(2)}, u32[]{:S(2)}) %collective-permute-start.6) | collective-permute-done | bytes 393248 | tf_op jit(solution)/shard_map/ppermute | solution.py:72
  145.4 4.8 %collective-permute-start.7 = (f32[2,192,256]{2,1,0:T(8,128)S(1)}, f32[2,192,256]{2,1,0:T(8,128)S(1)}, u32[]{:S(2)}, u32[]{:S(2)}) collective-permute-start(f32[2,192,256]{2,1,0:T(8,128)S(1)} %pad_maximum_fusion), channel_id=1, source_target_pairs={{0,1},{1,0},{2,3},{3,2},{4,5},{5,4},{6,7},{7,6},{8,9},{9,8},{10,11... | collective-permute-start | bytes 1179656 | tf_op jit(solution)/shard_map/ppermute | solution.py:72
  150.2 12.9 %all_to_all.22.pairs_ref = f32[24,2,192]{2,1,0:T(2,128)S(1)} all-to-all(f32[24,2,192]{2,1,0:T(2,128)S(1)} %get-tuple-element.13), channel_id=1, replica_groups=mesh['xh'=2,'yh'=4,'yl'=2,'zh'=6,'zl'=2,'xl'=2,'c'=2] {'zh','zl','c'}, dimensions={0} | all-to-all | bytes 73728 | tf_op jit(solution)/shard_map/all_to_all | solution.py:398
  163.1 0.1 merge.1
  163.2 14.6 %all_to_all.23.pairs_ref = f32[32,2,2,192]{3,2,1,0:T(2,128)S(1)} all-to-all(f32[32,2,2,192]{3,2,1,0:T(2,128)S(1)} %merge.1), channel_id=1, replica_groups=mesh['xh'=2,'yh'=4,'yl'=2,'zh'=6,'zl'=2,'xl'=2,'c'=2] {'xh','yh','yl','xl'}, dimensions={0} | all-to-all | bytes 196608 | tf_op jit(solution)/shard_map/all_to_all | solution.py:399
  177.8 1.4 finish.1
  179.2 0.0 collective-permute-done.7.given_ref
  179.2 1.3 arrange.1
  (3 shorter events, 0.1 us)
Async XLA Ops:
  0.6 66.6 %copy-start = (f32[4096]{0:T(1024)S(1)}, f32[4096]{0:T(1024)}, u32[]{:S(2)}) copy-start(f32[4096]{0:T(1024)} %param.13) | copy-start | bytes 49156
  0.6 41.1 %collective-permute-start.4 = (bf16[256,4096]{1,0:T(8,128)(2,1)}, bf16[256,4096]{1,0:T(8,128)(2,1)}, u32[]{:S(2)}, u32[]{:S(2)}) collective-permute-start(bf16[256,4096]{1,0:T(8,128)(2,1)} %refs_0_.3), channel_id=1, source_target_pairs={{0,2},{2,0},{1,3},{3,1},{4,6},{6,4},{5,7},{7,5},{8,10},{10,8},{9,1... | collective-permute-start | bytes 6291464 | tf_op jit(solution)/shard_map/ppermute | solution.py:72
  4.6 114.2 %collective-permute-start.3 = (bf16[256,4096]{1,0:T(8,128)(2,1)}, bf16[256,4096]{1,0:T(8,128)(2,1)}, u32[]{:S(2)}, u32[]{:S(2)}) collective-permute-start(bf16[256,4096]{1,0:T(8,128)(2,1)} %refs_0_.3), channel_id=1, source_target_pairs={{0,1},{1,0},{2,3},{3,2},{4,5},{5,4},{6,7},{7,6},{8,9},{9,8},{10,11... | collective-permute-start | bytes 6291464 | tf_op jit(solution)/shard_map/ppermute | solution.py:72
  41.7 89.9 %collective-permute-start.5 = (bf16[256,4096]{1,0:T(8,128)(2,1)}, bf16[256,4096]{1,0:T(8,128)(2,1)S(1)}, u32[]{:S(2)}, u32[]{:S(2)}) collective-permute-start(bf16[256,4096]{1,0:T(8,128)(2,1)} %collective-permute-done.4.refs_2_), channel_id=1, source_target_pairs={{0,1},{1,0},{2,3},{3,2},{4,5},{5,4},{6,7},{7,6},{8,9},{9,8},{10,11... | collective-permute-start | bytes 6291464 | tf_op jit(solution)/shard_map/ppermute | solution.py:72
  104.4 18.1 %collective-permute-start = (bf16[48,4096]{1,0:T(8,128)(2,1)S(1)}, bf16[48,4096]{1,0:T(8,128)(2,1)S(1)}, u32[]{:S(2)}, u32[]{:S(2)}) collective-permute-start(bf16[48,4096]{1,0:T(8,128)(2,1)S(1)} %reshape.11.refs_0_), channel_id=1, source_target_pairs={{0,44},{4,0},{8,4},{12,8},{16,12},{20,16},{24,20},{28,24},{32,28},... | collective-permute-start | bytes 1179656 | tf_op jit(solution)/shard_map/ppermute | solution.py:68
  115.0 11.4 %collective-permute-start.1 = (bf16[48,4096]{1,0:T(8,128)(2,1)S(1)}, bf16[48,4096]{1,0:T(8,128)(2,1)S(1)}, u32[]{:S(2)}, u32[]{:S(2)}) collective-permute-start(bf16[48,4096]{1,0:T(8,128)(2,1)S(1)} %reshape.11.refs_0_), channel_id=1, source_target_pairs={{0,336},{4,340},{8,344},{12,348},{16,352},{20,356},{24,360},{28,36... | collective-permute-start | bytes 1179656 | tf_op jit(solution)/shard_map/ppermute | solution.py:68
  116.9 14.7 %collective-permute-start.2 = (bf16[48,4096]{1,0:T(8,128)(2,1)S(1)}, bf16[48,4096]{1,0:T(8,128)(2,1)S(1)}, u32[]{:S(2)}, u32[]{:S(2)}) collective-permute-start(bf16[48,4096]{1,0:T(8,128)(2,1)S(1)} %reshape.11.refs_0_), channel_id=1, source_target_pairs={{0,52},{4,56},{8,60},{12,64},{16,68},{20,72},{24,76},{28,80},{32,8... | collective-permute-start | bytes 1179656 | tf_op jit(solution)/shard_map/ppermute | solution.py:68
  134.8 10.6 %collective-permute-start.6 = (f32[2,192,256]{2,1,0:T(8,128)S(1)}, f32[2,192,256]{2,1,0:T(8,128)S(1)}, u32[]{:S(2)}, u32[]{:S(2)}) collective-permute-start(f32[2,192,256]{2,1,0:T(8,128)S(1)} %get-tuple-element.12), channel_id=1, source_target_pairs={{0,2},{2,0},{1,3},{3,1},{4,6},{6,4},{5,7},{7,5},{8,10},{10,8},{9,1... | collective-permute-start | bytes 1179656 | tf_op jit(solution)/shard_map/ppermute | solution.py:72
  145.4 33.8 %collective-permute-start.7 = (f32[2,192,256]{2,1,0:T(8,128)S(1)}, f32[2,192,256]{2,1,0:T(8,128)S(1)}, u32[]{:S(2)}, u32[]{:S(2)}) collective-permute-start(f32[2,192,256]{2,1,0:T(8,128)S(1)} %pad_maximum_fusion), channel_id=1, source_target_pairs={{0,1},{1,0},{2,3},{3,2},{4,5},{5,4},{6,7},{7,6},{8,9},{9,8},{10,11... | collective-permute-start | bytes 1179656 | tf_op jit(solution)/shard_map/ppermute | solution.py:72

commit v6 on v5

--- a/solution.py
+++ b/solution.py
@@ -27,23 +27,24 @@
 def finish_kernel(sizes, pairs_ref, out_ref):
     xh, yh, yl, zh, zl, xl, c = sizes
     members, count = pairs_ref.shape[0] // xl, pairs_ref.shape[-1]
-    row = lax.broadcasted_iota(jnp.int32, (count, out_ref.shape[0]), 0)
+    row = lax.broadcasted_iota(jnp.int32, (count, 1), 0)
     x, z1, y1 = row % xh, row // xh % zh, row // (xh * zh) % yh
     z0, y0 = row // (xh * zh * yh) % zl, row // (xh * zh * yh * zl)
-    place = (((x * yh + y1) * yl + y0) * zh + z1) * zl + z0
-    target = lax.broadcasted_iota(jnp.int32, row.shape, 1)
-    out = jnp.zeros((1, out_ref.shape[0]), jnp.float32)
+    place = ((((x * yh + y1) * yl + y0) * zh + z1) * zl + z0) * (xl * c)
+    target = lax.broadcasted_iota(jnp.int32, (count, out_ref.shape[0]), 1)
+    term = lax.broadcasted_iota(jnp.int32, (8, count), 0)
+    out = jnp.zeros((8, out_ref.shape[0]), jnp.float32)
     for t in range(xl * c):
         peak, total = merged([pairs_ref[m * xl + t // c, t % c] for m in range(members)])
         value = peak + jnp.log(total)
-        high = value.astype(jnp.bfloat16)
-        rest = value - high.astype(jnp.float32)
-        middle = rest.astype(jnp.bfloat16)
-        low = (rest - middle.astype(jnp.float32)).astype(jnp.bfloat16)
-        chosen = jnp.where(place * (xl * c) + t == target, 1.0, 0.0).astype(jnp.bfloat16)
-        for term in (low, middle, high):
-            spread = jnp.broadcast_to(term.astype(jnp.float32), (8, count)).astype(jnp.bfloat16)
-            out = out + jnp.dot(spread, chosen, preferred_element_type=jnp.float32)[:1]
+        high = value.astype(jnp.bfloat16).astype(jnp.float32)
+        middle = (value - high).astype(jnp.bfloat16).astype(jnp.float32)
+        low = value - high - middle
+        terms = jnp.where(term == 0, high, jnp.where(term == 1, middle, low))
+        terms = jnp.where(term < 3, terms, 0.0).astype(jnp.bfloat16)
+        chosen = jnp.where(place + t == target, 1.0, 0.0).astype(jnp.bfloat16)
+        out = out + jnp.dot(terms, chosen, preferred_element_type=jnp.float32)
+    out = (out[2:3] + out[1:2]) + out[0:1]
     out_ref[...] = out[0]
 
 
@@ -166,7 +167,7 @@
 
 def project(q_states, k_states, v_states, residual, out_weight, lengths, total):
     depth, width = out_weight.shape
-    chunks = 4
+    chunks = 8
     whole = [q_states, k_states, v_states, residual]
     arrays = [
         pltpu.with_memory_space_constraint(x, pltpu.HBM) for x in (*whole, out_weight, lengths)

time: 181 us -> 181 us (level)
  no operation moved by 1% of the time
where the time goes in v6:
time: 181 us; the launch traced here: 180 us
  blocking collectives  74 us (41%)
  starting transfers between devices  47.4 us (26%)
  waiting for transfers between devices  45 us (25%)
  Pallas kernels  12.8 us (7%)
    all_to_all x1, blocking collectives, step(): lax.all_to_all(embed, (YH, ZH), 0, 0, tiled=True).reshape(-1, width)  36.8 us
    ppermute x5, waiting for transfers between devices, swap(): return lax.ppermute(array, axis, [(0, 1), (1, 0)])  35.1 us
    ppermute x5, starting transfers between devices, swap(): return lax.ppermute(array, axis, [(0, 1), (1, 0)])  33 us
    all_to_all x1, blocking collectives, step(): lax.all_to_all(merge(pairs, c, xh * yh * yl * xl), (XH, YH, YL, XL), 0, 0...  14.6 us
    ppermute x3, starting transfers between devices, shifted(): return lax.ppermute(array, axes, moves)  14.4 us
    all_to_all x1, blocking collectives, step(): pairs = lax.all_to_all(stats, (ZH, ZL, C), 0, 0, tiled=True)  12.9 us
    ppermute x3, waiting for transfers between devices, shifted(): return lax.ppermute(array, axes, moves)  9.89 us
    all_to_all x1, blocking collectives, step(): terms = lax.all_to_all(terms, (XH, XL, C), 0, 0, tiled=True)  9.69 us
  transfers between devices with their start and end apart: 8, of which 5 were waited for; matrix products, arithmetic and copies ran while one was open for 0% of the time, Pallas kernels for 5%

profile of v6, /device:TPU:1, one launch (start us, length us, event | category | flops | bytes accessed | tf_op | source)
XLA Modules:
  0.0 180.2 jit_solution(11830674897319454501)
XLA Ops:
  0.6 0.0 copy-start
  0.6 3.9 %collective-permute-start.4 = (bf16[256,4096]{1,0:T(8,128)(2,1)}, bf16[256,4096]{1,0:T(8,128)(2,1)}, u32[]{:S(2)}, u32[]{:S(2)}) collective-permute-start(bf16[256,4096]{1,0:T(8,128)(2,1)} %refs_0_.3), channel_id=1, source_target_pairs={{0,2},{2,0},{1,3},{3,1},{4,6},{6,4},{5,7},{7,5},{8,10},{10,8},{9,1... | collective-permute-start | bytes 6291464 | tf_op jit(solution)/shard_map/ppermute | solution.py:73
  4.6 10.4 %collective-permute-start.3 = (bf16[256,4096]{1,0:T(8,128)(2,1)}, bf16[256,4096]{1,0:T(8,128)(2,1)}, u32[]{:S(2)}, u32[]{:S(2)}) collective-permute-start(bf16[256,4096]{1,0:T(8,128)(2,1)} %refs_0_.3), channel_id=1, source_target_pairs={{0,1},{1,0},{2,3},{3,2},{4,5},{5,4},{6,7},{7,6},{8,9},{9,8},{10,11... | collective-permute-start | bytes 6291464 | tf_op jit(solution)/shard_map/ppermute | solution.py:73
  15.0 26.7 %collective-permute-done.4.refs_2_ = bf16[256,4096]{1,0:T(8,128)(2,1)} collective-permute-done((bf16[256,4096]{1,0:T(8,128)(2,1)}, bf16[256,4096]{1,0:T(8,128)(2,1)}, u32[]{:S(2)}, u32[]{:S(2)}) %collective-permute-start.4) | collective-permute-done | bytes 2097184 | tf_op jit(solution)/shard_map/ppermute | solution.py:73
  41.7 11.7 %collective-permute-start.5 = (bf16[256,4096]{1,0:T(8,128)(2,1)}, bf16[256,4096]{1,0:T(8,128)(2,1)S(1)}, u32[]{:S(2)}, u32[]{:S(2)}) collective-permute-start(bf16[256,4096]{1,0:T(8,128)(2,1)} %collective-permute-done.4.refs_2_), channel_id=1, source_target_pairs={{0,1},{1,0},{2,3},{3,2},{4,5},{5,4},{6,7},{7,6},{8,9},{9,8},{10,11... | collective-permute-start | bytes 6291464 | tf_op jit(solution)/shard_map/ppermute | solution.py:73
  53.4 4.0 %project.1 = f32[8,1,4096]{2,1,0:T(1,128)S(1)} custom-call(bf16[64,1024]{1,0:T(8,128)(2,1)} %refs_0_.2, bf16[64,256]{1,0:T(8,128)(2,1)} %refs_1_.1, bf16[64,256]{1,0:T(8,128)(2,1)} %refs_2_.1, bf16[64,4096]{1,0:T(8,128)(2,1)} %refs_3_.1, bf16[1024,4096]{1,0:T(8,128)(2,1)} %refs_4_.1, s32[4]{0:T(128)} %refs_5_.1), custom_call_target="tpu_custom_call" | custom-call | tf_op jit(solution)/shard_map/project/pallas_call | solution.py:175
  57.4 9.7 %all_to_all.20.terms_ref = f32[8,1,4096]{2,1,0:T(1,128)S(1)} all-to-all(f32[8,1,4096]{2,1,0:T(1,128)S(1)} %project.1), channel_id=1, replica_groups=mesh['xh'=2,'yh'=4,'yl'=2,'zh'=6,'zl'=2,'xl'=2,'c'=2] {'xh','xl','c'}, dimensions={0} | all-to-all | bytes 262144 | tf_op jit(solution)/shard_map/all_to_all | solution.py:376
  67.1 0.0 copy-done
  67.1 0.2 embed_rows.1
  67.3 36.8 %all_to_all.21 = bf16[24,2,4096]{2,1,0:T(2,128)(2,1)S(1)} all-to-all(bf16[24,2,4096]{2,1,0:T(2,128)(2,1)S(1)} %embed_rows.1), channel_id=1, replica_groups=mesh['xh'=2,'yh'=4,'yl'=2,'zh'=6,'zl'=2,'xl'=2,'c'=2] {'yh','zh'}, dimensions={0} | all-to-all | bytes 786432 | tf_op jit(solution)/shard_map/all_to_all | solution.py:383
  104.1 0.1 reshape.11.refs_0_
  104.2 10.6 %collective-permute-start = (bf16[48,4096]{1,0:T(8,128)(2,1)S(1)}, bf16[48,4096]{1,0:T(8,128)(2,1)S(1)}, u32[]{:S(2)}, u32[]{:S(2)}) collective-permute-start(bf16[48,4096]{1,0:T(8,128)(2,1)S(1)} %reshape.11.refs_0_), channel_id=1, source_target_pairs={{0,44},{4,0},{8,4},{12,8},{16,12},{20,16},{24,20},{28,24},{32,28},... | collective-permute-start | bytes 1179656 | tf_op jit(solution)/shard_map/ppermute | solution.py:69
  114.8 1.9 %collective-permute-start.1 = (bf16[48,4096]{1,0:T(8,128)(2,1)S(1)}, bf16[48,4096]{1,0:T(8,128)(2,1)S(1)}, u32[]{:S(2)}, u32[]{:S(2)}) collective-permute-start(bf16[48,4096]{1,0:T(8,128)(2,1)S(1)} %reshape.11.refs_0_), channel_id=1, source_target_pairs={{0,336},{4,340},{8,344},{12,348},{16,352},{20,356},{24,360},{28,36... | collective-permute-start | bytes 1179656 | tf_op jit(solution)/shard_map/ppermute | solution.py:69
  116.7 1.9 %collective-permute-start.2 = (bf16[48,4096]{1,0:T(8,128)(2,1)S(1)}, bf16[48,4096]{1,0:T(8,128)(2,1)S(1)}, u32[]{:S(2)}, u32[]{:S(2)}) collective-permute-start(bf16[48,4096]{1,0:T(8,128)(2,1)S(1)} %reshape.11.refs_0_), channel_id=1, source_target_pairs={{0,52},{4,56},{8,60},{12,64},{16,68},{20,72},{24,76},{28,80},{32,8... | collective-permute-start | bytes 1179656 | tf_op jit(solution)/shard_map/ppermute | solution.py:69
  118.7 0.0 collective-permute-done.3.refs_1_
  118.7 2.9 %hold.1 = (bf16[256,4096]{1,0:T(8,128)(2,1)S(1)}, bf16[256,4096]{1,0:T(8,128)(2,1)S(1)}, bf16[256,4096]{1,0:T(8,128)(2,1)S(1)}) custom-call(bf16[256,4096]{1,0:T(8,128)(2,1)} %refs_0_.3, bf16[256,4096]{1,0:T(8,128)(2,1)} %collective-permute-done.3.refs_1_, bf16[256,4096]{1,0:T(8,128)(2,1)} %collective-permute-done.4.refs_2_), custom_call_target="tpu_custom_call" | custom-call | flops 1 | bytes 12582912 | tf_op jit(solution)/shard_map/hold/pallas_call | solution.py:292
  121.6 0.8 collective-permute-done.refs_1_
  122.4 3.8 %collective-permute-done.1.refs_2_ = bf16[48,4096]{1,0:T(8,128)(2,1)S(1)} collective-permute-done((bf16[48,4096]{1,0:T(8,128)(2,1)S(1)}, bf16[48,4096]{1,0:T(8,128)(2,1)S(1)}, u32[]{:S(2)}, u32[]{:S(2)}) %collective-permute-start.1) | collective-permute-done | bytes 393248 | tf_op jit(solution)/shard_map/ppermute | solution.py:69
  126.2 5.2 %collective-permute-done.2.refs_3_ = bf16[48,4096]{1,0:T(8,128)(2,1)S(1)} collective-permute-done((bf16[48,4096]{1,0:T(8,128)(2,1)S(1)}, bf16[48,4096]{1,0:T(8,128)(2,1)S(1)}, u32[]{:S(2)}, u32[]{:S(2)}) %collective-permute-start.2) | collective-permute-done | bytes 393248 | tf_op jit(solution)/shard_map/ppermute | solution.py:69
  131.5 0.0 collective-permute-done.5.refs_7_
  131.5 3.2 %score_blocks.1 = (f32[2,192,256]{2,1,0:T(8,128)S(1)}, f32[2,192,256]{2,1,0:T(8,128)S(1)}, f32[24,2,192]{2,1,0:T(2,128)S(1)}) custom-call(bf16[48,4096]{1,0:T(8,128)(2,1)S(1)} %reshape.11.refs_0_, bf16[48,4096]{1,0:T(8,128)(2,1)S(1)} %collective-permute-done.refs_1_, bf16[48,4096]{1,0:T(8,128)(2,1)S(1)} %collective-permute-done.1.refs_2_, ...), custom_call_target="tpu_custom_call" | custom-call | flops 1610612736 | bytes 8388608 | tf_op jit(solution)/shard_map/score_blocks/pallas_call | solution.py:312
  134.6 2.2 %collective-permute-start.6 = (f32[2,192,256]{2,1,0:T(8,128)S(1)}, f32[2,192,256]{2,1,0:T(8,128)S(1)}, u32[]{:S(2)}, u32[]{:S(2)}) collective-permute-start(f32[2,192,256]{2,1,0:T(8,128)S(1)} %get-tuple-element.12), channel_id=1, source_target_pairs={{0,2},{2,0},{1,3},{3,1},{4,6},{6,4},{5,7},{7,5},{8,10},{10,8},{9,1... | collective-permute-start | bytes 1179656 | tf_op jit(solution)/shard_map/ppermute | solution.py:73
  136.9 8.3 %collective-permute-done.6.crossed_ref = f32[2,192,256]{2,1,0:T(8,128)S(1)} collective-permute-done((f32[2,192,256]{2,1,0:T(8,128)S(1)}, f32[2,192,256]{2,1,0:T(8,128)S(1)}, u32[]{:S(2)}, u32[]{:S(2)}) %collective-permute-start.6) | collective-permute-done | bytes 393248 | tf_op jit(solution)/shard_map/ppermute | solution.py:73
  145.3 4.8 %collective-permute-start.7 = (f32[2,192,256]{2,1,0:T(8,128)S(1)}, f32[2,192,256]{2,1,0:T(8,128)S(1)}, u32[]{:S(2)}, u32[]{:S(2)}) collective-permute-start(f32[2,192,256]{2,1,0:T(8,128)S(1)} %pad_maximum_fusion), channel_id=1, source_target_pairs={{0,1},{1,0},{2,3},{3,2},{4,5},{5,4},{6,7},{7,6},{8,9},{9,8},{10,11... | collective-permute-start | bytes 1179656 | tf_op jit(solution)/shard_map/ppermute | solution.py:73
  150.0 12.9 %all_to_all.22.pairs_ref = f32[24,2,192]{2,1,0:T(2,128)S(1)} all-to-all(f32[24,2,192]{2,1,0:T(2,128)S(1)} %get-tuple-element.13), channel_id=1, replica_groups=mesh['xh'=2,'yh'=4,'yl'=2,'zh'=6,'zl'=2,'xl'=2,'c'=2] {'zh','zl','c'}, dimensions={0} | all-to-all | bytes 73728 | tf_op jit(solution)/shard_map/all_to_all | solution.py:399
  163.0 0.1 merge.1
  163.0 14.6 %all_to_all.23.pairs_ref = f32[32,2,2,192]{3,2,1,0:T(2,128)S(1)} all-to-all(f32[32,2,2,192]{3,2,1,0:T(2,128)S(1)} %merge.1), channel_id=1, replica_groups=mesh['xh'=2,'yh'=4,'yl'=2,'zh'=6,'zl'=2,'xl'=2,'c'=2] {'xh','yh','yl','xl'}, dimensions={0} | all-to-all | bytes 196608 | tf_op jit(solution)/shard_map/all_to_all | solution.py:400
  177.7 1.2 finish.1
  178.9 0.0 collective-permute-done.7.given_ref
  178.9 1.3 arrange.1
  (3 shorter events, 0.1 us)
Async XLA Ops:
  0.6 66.5 %copy-start = (f32[4096]{0:T(1024)S(1)}, f32[4096]{0:T(1024)}, u32[]{:S(2)}) copy-start(f32[4096]{0:T(1024)} %param.13) | copy-start | bytes 49156
  0.6 41.1 %collective-permute-start.4 = (bf16[256,4096]{1,0:T(8,128)(2,1)}, bf16[256,4096]{1,0:T(8,128)(2,1)}, u32[]{:S(2)}, u32[]{:S(2)}) collective-permute-start(bf16[256,4096]{1,0:T(8,128)(2,1)} %refs_0_.3), channel_id=1, source_target_pairs={{0,2},{2,0},{1,3},{3,1},{4,6},{6,4},{5,7},{7,5},{8,10},{10,8},{9,1... | collective-permute-start | bytes 6291464 | tf_op jit(solution)/shard_map/ppermute | solution.py:73
  4.6 114.1 %collective-permute-start.3 = (bf16[256,4096]{1,0:T(8,128)(2,1)}, bf16[256,4096]{1,0:T(8,128)(2,1)}, u32[]{:S(2)}, u32[]{:S(2)}) collective-permute-start(bf16[256,4096]{1,0:T(8,128)(2,1)} %refs_0_.3), channel_id=1, source_target_pairs={{0,1},{1,0},{2,3},{3,2},{4,5},{5,4},{6,7},{7,6},{8,9},{9,8},{10,11... | collective-permute-start | bytes 6291464 | tf_op jit(solution)/shard_map/ppermute | solution.py:73
  41.7 89.8 %collective-permute-start.5 = (bf16[256,4096]{1,0:T(8,128)(2,1)}, bf16[256,4096]{1,0:T(8,128)(2,1)S(1)}, u32[]{:S(2)}, u32[]{:S(2)}) collective-permute-start(bf16[256,4096]{1,0:T(8,128)(2,1)} %collective-permute-done.4.refs_2_), channel_id=1, source_target_pairs={{0,1},{1,0},{2,3},{3,2},{4,5},{5,4},{6,7},{7,6},{8,9},{9,8},{10,11... | collective-permute-start | bytes 6291464 | tf_op jit(solution)/shard_map/ppermute | solution.py:73
  104.2 18.1 %collective-permute-start = (bf16[48,4096]{1,0:T(8,128)(2,1)S(1)}, bf16[48,4096]{1,0:T(8,128)(2,1)S(1)}, u32[]{:S(2)}, u32[]{:S(2)}) collective-permute-start(bf16[48,4096]{1,0:T(8,128)(2,1)S(1)} %reshape.11.refs_0_), channel_id=1, source_target_pairs={{0,44},{4,0},{8,4},{12,8},{16,12},{20,16},{24,20},{28,24},{32,28},... | collective-permute-start | bytes 1179656 | tf_op jit(solution)/shard_map/ppermute | solution.py:69
  114.8 11.4 %collective-permute-start.1 = (bf16[48,4096]{1,0:T(8,128)(2,1)S(1)}, bf16[48,4096]{1,0:T(8,128)(2,1)S(1)}, u32[]{:S(2)}, u32[]{:S(2)}) collective-permute-start(bf16[48,4096]{1,0:T(8,128)(2,1)S(1)} %reshape.11.refs_0_), channel_id=1, source_target_pairs={{0,336},{4,340},{8,344},{12,348},{16,352},{20,356},{24,360},{28,36... | collective-permute-start | bytes 1179656 | tf_op jit(solution)/shard_map/ppermute | solution.py:69
  116.7 14.7 %collective-permute-start.2 = (bf16[48,4096]{1,0:T(8,128)(2,1)S(1)}, bf16[48,4096]{1,0:T(8,128)(2,1)S(1)}, u32[]{:S(2)}, u32[]{:S(2)}) collective-permute-start(bf16[48,4096]{1,0:T(8,128)(2,1)S(1)} %reshape.11.refs_0_), channel_id=1, source_target_pairs={{0,52},{4,56},{8,60},{12,64},{16,68},{20,72},{24,76},{28,80},{32,8... | collective-permute-start | bytes 1179656 | tf_op jit(solution)/shard_map/ppermute | solution.py:69
  134.6 10.6 %collective-permute-start.6 = (f32[2,192,256]{2,1,0:T(8,128)S(1)}, f32[2,192,256]{2,1,0:T(8,128)S(1)}, u32[]{:S(2)}, u32[]{:S(2)}) collective-permute-start(f32[2,192,256]{2,1,0:T(8,128)S(1)} %get-tuple-element.12), channel_id=1, source_target_pairs={{0,2},{2,0},{1,3},{3,1},{4,6},{6,4},{5,7},{7,5},{8,10},{10,8},{9,1... | collective-permute-start | bytes 1179656 | tf_op jit(solution)/shard_map/ppermute | solution.py:73
  145.3 33.6 %collective-permute-start.7 = (f32[2,192,256]{2,1,0:T(8,128)S(1)}, f32[2,192,256]{2,1,0:T(8,128)S(1)}, u32[]{:S(2)}, u32[]{:S(2)}) collective-permute-start(f32[2,192,256]{2,1,0:T(8,128)S(1)} %pad_maximum_fusion), channel_id=1, source_target_pairs={{0,1},{1,0},{2,3},{3,2},{4,5},{5,4},{6,7},{7,6},{8,9},{9,8},{10,11... | collective-permute-start | bytes 1179656 | tf_op jit(solution)/shard_map/ppermute | solution.py:73
